TPU v7x, 128 devices: a whole 4x4x4 slice. The times are simulated.
128 devices in a mesh: bngroup: 8 (over z, core), rep: 16 (over x, y).
Axes of the slice: x: 4, y: 4, z: 4, core: 2. Of those that a mesh axis runs over, the one named last changes fastest.
Arguments:
- images: bfloat16 [1536, 7, 7, 2048], P(('bngroup', 'rep')), may hold values from -12 to 12
- cotangent: bfloat16 [1536, 7, 7, 2048], P(('bngroup', 'rep')), may hold values from -6 to 6
- w_reduce: bfloat16 [2048, 512], replicated, may hold values from -0.125 to 0.125
- w_spatial: bfloat16 [4608, 512], replicated, may hold values from -0.09375 to 0.09375
- w_expand: bfloat16 [2048, 512], replicated, may hold values from -0.25 to 0.25
- norm_gain: float32 [3072], replicated, may hold values from 0.25 to 1.75
- norm_shift: float32 [3072], replicated, may hold values from -3 to 3
Outputs:
- output: bfloat16 [1536, 7, 7, 2048], P(('bngroup', 'rep'))
- in_grad: bfloat16 [1536, 7, 7, 2048], P(('bngroup', 'rep'))
- weight_grads: float32 [8704, 512], P('bngroup', 'rep')
- norm_grads: float32 [2, 3072], replicated
All inputs are finite; a program needn't handle non-finite values.
Results may differ from a plain program's by a relative error of at most 0.007.
Values sent between devices are 32-bit elements.
A program may use at most 192 MiB of HBM per device.

v0:
```python
import jax
import jax.numpy as jnp
from jax import lax
from jax.sharding import Mesh
from jax.sharding import PartitionSpec as P

BNGROUP = ("bngroup_0", "bngroup_1")
REP = ("rep_0", "rep_1")
BNGROUP_REP = ("bngroup_0", "bngroup_1", "rep_0", "rep_1")


EPS = 0.25


def from_everyone(value, axis):
    devices = lax.axis_size(axis)
    return lax.all_to_all(
        jnp.broadcast_to(value[None], (devices, *value.shape)), axis, 0, 0, tiled=True
    )


def of_everyone(value, axis):
    everything = from_everyone(value, axis)
    return jnp.sum(everything, axis=0)


def packed_total(arrays, axis):
    ends = [0]
    for a in arrays:
        ends.append(ends[-1] + a.size)
    total = of_everyone(jnp.concatenate([a.ravel() for a in arrays]), axis)
    return tuple((total[b:e].reshape(a.shape) for a, b, e in zip(arrays, ends, ends[1:])))


def by_axis(value, axes):
    for axis in axes:
        value = lax.psum(value, axis)
    return value


def in_blocks(value, dim, devices):
    before, after = (value.shape[:dim], value.shape[dim + 1 :])
    return jnp.moveaxis(value.reshape(*before, devices, -1, *after), dim, 0)


def sum_at_owner(value, axis, dim):
    devices = lax.axis_size(axis)
    blocks = lax.all_to_all(in_blocks(value, dim, devices), axis, 0, 0, tiled=True)
    return jnp.sum(blocks, axis=0)


def matmul(left, right):
    return jnp.dot(left, right, preferred_element_type=jnp.float32)


def contract(left, right, left_dim, right_dim):
    return lax.dot_general(
        left, right, (((left_dim,), (right_dim,)), ((), ())), preferred_element_type=jnp.float32
    )


def slope(value):
    sigma = jax.nn.sigmoid(value)
    return sigma * (1.0 + value * (1.0 - sigma))


def normalize(pre_norm, norm_gain, norm_shift, group_size):
    number = pre_norm.shape[0] * group_size
    first_sum, second_sum = packed_total(
        (jnp.sum(pre_norm, axis=0), jnp.sum(pre_norm * pre_norm, axis=0)), BNGROUP
    )
    centre = first_sum / number
    spread = jnp.maximum(second_sum / number - centre * centre, 0.0)
    inverse = lax.rsqrt(spread + EPS)
    scaled = (pre_norm - centre) * inverse
    return (scaled, inverse, norm_gain * scaled + norm_shift)


def norm_back(upstream, scaled, inverse, norm_gain, group_size):
    shift_sum, gain_sum = (
        by_axis(jnp.sum(upstream, axis=0), BNGROUP),
        by_axis(jnp.sum(upstream * scaled, axis=0), BNGROUP),
    )
    number = upstream.shape[0] * group_size
    result = norm_gain * inverse * (upstream - shift_sum / number - scaled * gain_sum / number)
    return (result.astype(jnp.bfloat16), shift_sum, gain_sum)


def unfold(field):
    length = field.shape[1]
    padded = jnp.pad(field, ((0, 0), (1, 1), (1, 1), (0, 0)))
    windows = [
        padded[:, row_tap : row_tap + length, col_tap : col_tap + length, :]
        for row_tap in range(3)
        for col_tap in range(3)
    ]
    return jnp.concatenate(windows, axis=-1).reshape(-1, 9 * field.shape[3])


def fold_back(columns, images_count, length, channels):
    shaped = columns.reshape(images_count, length, length, 9, channels)
    summed = jnp.zeros((images_count, length + 2, length + 2, channels), jnp.float32)
    for row_tap in range(3):
        for col_tap in range(3):
            summed = summed + jnp.pad(
                shaped[:, :, :, 3 * row_tap + col_tap, :],
                ((0, 0), (row_tap, 2 - row_tap), (col_tap, 2 - col_tap), (0, 0)),
            )
    return summed[:, 1 : length + 1, 1 : length + 1, :].reshape(-1, channels)


def per_device(images, cotangent, w_reduce, w_spatial, w_expand, norm_gain, norm_shift):
    group_size = lax.axis_size(BNGROUP)
    images_total = images.shape[0] * group_size * lax.axis_size(REP)
    images_count = images.shape[0]
    length = images.shape[1]
    wide_ch = images.shape[3]
    mid_ch = w_reduce.shape[1]
    flat_in = images.reshape(-1, wide_ch)
    gain_one, gain_two, gain_three = (
        norm_gain[:mid_ch],
        norm_gain[mid_ch : 2 * mid_ch],
        norm_gain[2 * mid_ch :],
    )
    shift_one, shift_two, shift_three = (
        norm_shift[:mid_ch],
        norm_shift[mid_ch : 2 * mid_ch],
        norm_shift[2 * mid_ch :],
    )
    scaled_one, inverse_one, normed_one = normalize(
        matmul(flat_in, w_reduce), gain_one, shift_one, group_size
    )
    hidden_one = jax.nn.silu(normed_one).astype(jnp.bfloat16)
    patches = unfold(hidden_one.reshape(images_count, length, length, mid_ch))
    scaled_two, inverse_two, normed_two = normalize(
        matmul(patches, w_spatial), gain_two, shift_two, group_size
    )
    hidden_two = jax.nn.silu(normed_two).astype(jnp.bfloat16)
    scaled_three, inverse_three, normed_three = normalize(
        contract(hidden_two, w_expand, 1, 1), gain_three, shift_three, group_size
    )
    summed_in = normed_three + flat_in.astype(jnp.float32)
    output = jax.nn.silu(summed_in).astype(jnp.bfloat16)
    upstream = cotangent.reshape(-1, wide_ch).astype(jnp.float32) * slope(summed_in)
    grad_three, shift_sum_three, gain_sum_three = norm_back(
        upstream, scaled_three, inverse_three, gain_three, group_size
    )
    back_two = matmul(grad_three, w_expand) * slope(normed_two)
    grad_two, shift_sum_two, gain_sum_two = norm_back(
        back_two, scaled_two, inverse_two, gain_two, group_size
    )
    back_one = fold_back(contract(grad_two, w_spatial, 1, 1), images_count, length, mid_ch) * slope(
        normed_one
    )
    grad_one, shift_sum_one, gain_sum_one = norm_back(
        back_one, scaled_one, inverse_one, gain_one, group_size
    )
    in_grad = (upstream + contract(grad_one, w_reduce, 1, 1)).astype(jnp.bfloat16)
    local_grads = jnp.concatenate(
        [
            contract(flat_in, grad_one, 0, 0),
            contract(patches, grad_two, 0, 0),
            contract(grad_three, hidden_two, 0, 0),
        ],
        axis=0,
    )
    partial_grads = lax.psum_scatter(local_grads, BNGROUP, scatter_dimension=0, tiled=True)
    summed_grads = sum_at_owner(partial_grads, REP, 1)
    group_norms = jnp.stack(
        [
            jnp.concatenate([gain_sum_one, gain_sum_two, gain_sum_three]),
            jnp.concatenate([shift_sum_one, shift_sum_two, shift_sum_three]),
        ]
    )
    norm_summed = by_axis(group_norms, REP)
    return (
        output.reshape(images.shape),
        in_grad.reshape(images.shape),
        summed_grads / images_total,
        norm_summed / images_total,
    )


def solution(mesh):
    split = Mesh(mesh.devices.reshape(4, 2, 4, 4), ("bngroup_0", "bngroup_1", "rep_0", "rep_1"))
    in_specs = (
        P(BNGROUP_REP, None, None, None),
        P(BNGROUP_REP, None, None, None),
        P(),
        P(),
        P(),
        P(),
        P(),
    )
    out_specs = (
        P(BNGROUP_REP, None, None, None),
        P(BNGROUP_REP, None, None, None),
        P(BNGROUP, REP),
        P(),
    )
    return jax.shard_map(
        per_device, mesh=split, in_specs=in_specs, out_specs=out_specs, check_vma=False
    )
```

profile of v0, /device:TPU:0, one launch (start us, length us, event | category | flops | bytes accessed | tf_op | source)
XLA Modules:
  0.0 429.9 jit_solution(1024485865159037116)
XLA Ops:
  7.2 4.4 %reshape.82 = bf16[588,2048]{1,0:T(8,128)(2,1)} reshape(bf16[12,7,7,2048]{3,2,1,0:T(8,128)(2,1)} %param.7) | data formatting | bytes 4816896 | tf_op jit(solution)/shard_map/reshape | solution.py:119
  16.0 5.4 %all-to-all-start = ((f32[8,1,1024]{2,1,0:T(1,128)}), f32[8,1,1024]{2,1,0:T(1,128)S(1)}, u32[]{:S(2)}, u32[]{:S(2)}) async-start(f32[8,1,1024]{2,1,0:T(1,128)} %broadcast_in_dim.6), calls=%async_computation | async-start | bytes 65536 | tf_op jit(solution)/shard_map/all_to_all | solution.py:17
  21.4 5.4 %all-to-all-done = f32[8,1,1024]{2,1,0:T(1,128)S(1)} async-done(((f32[8,1,1024]{2,1,0:T(1,128)}), f32[8,1,1024]{2,1,0:T(1,128)S(1)}, u32[]{:S(2)}, u32[]{:S(2)}) %all-to-all-start) | async-done | bytes 32800 | tf_op jit(solution)/shard_map/all_to_all | solution.py:17
  30.2 6.1 %pad_slice_fusion = (bf16[12,7,7,512]{3,2,1,0:T(8,128)(2,1)}, bf16[12,7,7,512]{3,2,1,0:T(8,128)(2,1)}, bf16[12,7,7,512]{3,2,1,0:T(8,128)(2,1)}, bf16[12,7,7,512]...) fusion(bf16[12,7,7,512]{3,2,1,0:T(8,128)(2,1)} %reshape.83), kind=kLoop, calls=%fused_computation.10 | loop fusion | bytes 5419008 | tf_op jit(solution)/shard_map/slice | solution.py:93
  64.8 7.9 %fusion.13 = (f32[512]{0:T(512)S(1)}, f32[512]{0:T(512)S(1)}, f32[588,512]{1,0:T(8,128)}) fusion(bf16[588,4608]{1,0:T(8,128)(2,1)} %constant_dynamic-update-slice_fusion, bf16[4608,512]{1,0:T(8,128)(2,1)} %param.10), kind=kOutput, calls=%fused_computation.92 | convolution fusion | flops 2775434240 | bytes 11345920 | tf_op jit(solution)/shard_map/dot_general | solution.py:53
  72.7 7.8 %all_to_all.23 = f32[8,1,1024]{2,1,0:T(1,128)S(1)} all-to-all(f32[8,1,1024]{2,1,0:T(1,128)S(1)} %broadcast_in_dim.7), channel_id=1, replica_groups=mesh['bngroup_0'=4,'bngroup_1'=2,'rep_0'=4,'rep_1'=4] {'bngroup_0','bngr..., dimensions={0} | all-to-all | bytes 65536 | tf_op jit(solution)/shard_map/all_to_all | solution.py:17
  80.6 5.1 %fusion.10 = (f32[2048]{0:T(1024)S(1)}, f32[2048]{0:T(1024)S(1)}, f32[588,2048]{1,0:T(8,128)}) fusion(bf16[2048,512]{1,0:T(8,128)(2,1)S(1)} %copy-done, f32[588,512]{1,0:T(8,128)} %get-tuple-element.62, f32[512]{0:T(512)S(1)} %get-tuple-element.55, f32[512]{0:T(512)S(1)} %get-tuple-element.58, f32[512]{0:T(512)S(1)} %get-tuple-element.57, ...), kind=kOutput, calls=%fused_computation.89 | convolution fusion | flops 1239443456 | bytes 8142848 | tf_op jit(solution)/shard_map/dot_general | solution.py:57
  89.9 4.6 %reshape.89 = f32[588,2048]{1,0:T(8,128)} reshape(bf16[12,7,7,2048]{3,2,1,0:T(8,128)(2,1)} %param.8) | data formatting | bytes 7225344 | tf_op jit(solution)/shard_map/convert_element_type | solution.py:144
  96.0 7.9 %fusion.9 = (f32[2048]{0:T(1024)S(1)}, f32[2048]{0:T(1024)S(1)}, f32[588,2048]{1,0:T(8,128)}, bf16[588,2048]{1,0:T(8,128)(2,1)}) fusion(f32[2048]{0:T(1024)S(1)} %get-tuple-element.50, f32[588,2048]{1,0:T(8,128)} %get-tuple-element.63, f32[2048]{0:T(1024)S(1)} %get-tuple-element.49, f32[588,2048]{1,0:T(8,128)} %reshape.89, bf16[588,2048]{1,0:T(8,128)(2,1)} %reshape.82, ...), kind=kLoop, calls=%fused_computation.88 | loop fusion | flops 22876160 | bytes 19316736 | tf_op jit(solution)/shard_map/reduce_sum | solution.py:81
  103.8 15.9 %all-reduce.12 = (f32[2048]{0:T(1024)S(1)}, f32[2048]{0:T(1024)S(1)}) all-reduce(f32[2048]{0:T(1024)S(1)} %get-tuple-element.5, f32[2048]{0:T(1024)S(1)} %get-tuple-element.4), channel_id=1, replica_groups=mesh['bngroup_0'=4,'bngroup_1'=2,'rep_0'=4,'rep_1'=4] {'bngroup_0'}, use_global_device_ids=true, to_apply=%region_13.14 | all-reduce | flops 4096 | bytes 32768 | tf_op jit(solution)/shard_map/psum | solution.py:37
  123.2 5.2 %multiply_convert_fusion = bf16[588,2048]{1,0:T(8,128)(2,1)S(1)} fusion(f32[588,2048]{1,0:T(8,128)} %get-tuple-element.29, f32[588,2048]{1,0:T(8,128)} %get-tuple-element.63, f32[2048]{0:T(1024)S(1)} %get-tuple-element.26, f32[2048]{0:T(1024)S(1)} %broadcast_multiply_fusion.2, f32[2048]{0:T(1024)S(1)} %get-tuple-element.48, f32[2048]{0:T(1024)S(1)} %get-tuple-element.50, ...), kind=kLoop, calls=%fused_computation.2 | loop fusion | flops 9633792 | bytes 12083200 | tf_op jit(solution)/shard_map/convert_element_type | solution.py:86
  131.4 7.7 %all-reduce.11 = (f32[512]{0:T(512)S(1)}, f32[512]{0:T(512)S(1)}) all-reduce(f32[512]{0:T(512)S(1)} %get-tuple-element.11, f32[512]{0:T(512)S(1)} %get-tuple-element.10), channel_id=1, replica_groups=mesh['bngroup_0'=4,'bngroup_1'=2,'rep_0'=4,'rep_1'=4] {'bngroup_0'}, use_global_device_ids=true, to_apply=%region_19.20 | all-reduce | flops 1024 | bytes 8192 | tf_op jit(solution)/shard_map/psum | solution.py:37
  143.7 8.1 %fusion.17 = f32[588,4608]{1,0:T(8,128)} fusion(bf16[588,512]{1,0:T(8,128)(2,1)S(1)} %multiply_convert_fusion.3, bf16[4608,512]{1,0:T(8,128)(2,1)} %param.10), kind=kOutput, calls=%fused_computation.96 | convolution fusion | flops 2774532096 | bytes 16158720 | tf_op jit(solution)/shard_map/dot_general | solution.py:57
  151.8 6.3 %fusion.18 = f32[4608,512]{1,0:T(8,128)} fusion(bf16[588,4608]{1,0:T(8,128)(2,1)S(1)} %bitcast.61, bf16[588,512]{1,0:T(8,128)(2,1)S(1)} %multiply_convert_fusion.3), kind=kOutput, calls=%fused_computation.97 | convolution fusion | flops 2774532096 | bytes 15458304 | tf_op jit(solution)/shard_map/dot_general | solution.py:57
  162.2 14.0 %reshape.85 = f32[12,7,7,9,512]{4,3,2,1,0:T(8,128)} reshape(f32[588,4608]{1,0:T(8,128)} %fusion.17) | data formatting | bytes 21676032 | tf_op jit(solution)/shard_map/reshape | solution.py:101
  176.1 32.4 %fusion.15 = (f32[12,7,7,1,512]{4,3,2,1,0:T(1,128)}, f32[12,7,7,1,512]{4,3,2,1,0:T(1,128)}, f32[12,7,7,1,512]{4,3,2,1,0:T(1,128)}, f32[12,7,7,1,512]{4,3,2,1,0:T...) fusion(f32[12,7,7,9,512]{4,3,2,1,0:T(8,128)} %reshape.85), kind=kLoop, calls=%fused_computation.94 | loop fusion | bytes 21676032 | tf_op jit(solution)/shard_map/slice | solution.py:106
  220.8 9.8 %all-reduce.10 = (f32[512]{0:T(512)S(1)}, f32[512]{0:T(512)S(1)}) all-reduce(f32[512]{0:T(512)S(1)} %get-tuple-element.9, f32[512]{0:T(512)S(1)} %get-tuple-element.8), channel_id=1, replica_groups=mesh['bngroup_0'=4,'bngroup_1'=2,'rep_0'=4,'rep_1'=4] {'bngroup_0'}, use_global_device_ids=true, to_apply=%region_25.26 | all-reduce | flops 1024 | bytes 8192 | tf_op jit(solution)/shard_map/psum | solution.py:37
  238.5 5.3 %copy.52 = f32[2048,512]{1,0:T(8,128)} copy(f32[2048,512]{0,1:T(8,128)} %convolution_bitcast_fusion) | data formatting | bytes 8388608 | tf_op jit(solution)/shard_map/dot_general | solution.py:57
  243.9 14.6 %pad_maximum_fusion = f32[8704,512]{1,0:T(8,128)} fusion(f32[2048,512]{1,0:T(8,128)} %fusion.7, f32[4608,512]{1,0:T(8,128)} %fusion.18, f32[2048,512]{1,0:T(8,128)} %copy.52), kind=kLoop, calls=%fused_computation | loop fusion | flops 8912896 | bytes 35651584 | tf_op jit(solution)/shard_map/concatenate | solution.py:159
  258.5 96.3 %reduce-scatter.2.cloned.1.call-done = f32[1088,512]{1,0:T(8,128)} async-done(((f32[8704,512]{1,0:T(8,128)}), f32[1088,512]{1,0:T(8,128)}) %reduce-scatter.2.cloned.1.call-update) | async-done | bytes 2228240 | tf_op jit(solution)/shard_map/reduce_scatter | solution.py:167
  357.9 6.9 %all-to-all-start.3 = ((f32[16,1088,32]{1,2,0:T(8,128)}), f32[16,1088,32]{1,2,0:T(8,128)}, u32[]{:S(2)}, u32[]{:S(2)}) async-start(f32[16,1088,32]{1,2,0:T(8,128)} %bitcast.50), calls=%async_computation.4 | async-start | bytes 4718592 | tf_op jit(solution)/shard_map/all_to_all | solution.py:48
  364.7 5.9 %add_convert_fusion = bf16[588,2048]{1,0:T(8,128)(2,1)} fusion(f32[588,2048]{1,0:T(8,128)} %get-tuple-element.29, bf16[588,512]{1,0:T(8,128)(2,1)S(1)} %multiply_convert_fusion.2, bf16[2048,512]{1,0:T(8,128)(2,1)} %param.9), kind=kOutput, calls=%fused_computation.1 | convolution fusion | flops 1235533824 | bytes 9924608 | tf_op jit(solution)/shard_map/dot_general | solution.py:57
  379.1 22.8 %psum.110 = f32[2,3072]{1,0:T(2,128)S(1)} all-reduce(f32[2,3072]{1,0:T(2,128)S(1)} %pad_maximum_fusion.1), channel_id=1, replica_groups=mesh['bngroup_0'=4,'bngroup_1'=2,'rep_0'=4,'rep_1'=4] {'rep_0'}, use_global_device_ids=true, to_apply=%region_29.30 | all-reduce | flops 6144 | bytes 49152 | tf_op jit(solution)/shard_map/psum | solution.py:37
  401.9 18.0 %psum.111 = f32[2,3072]{1,0:T(2,128)S(1)} all-reduce(f32[2,3072]{1,0:T(2,128)S(1)} %psum.110), channel_id=1, replica_groups=mesh['bngroup_0'=4,'bngroup_1'=2,'rep_0'=4,'rep_1'=4] {'rep_1'}, use_global_device_ids=true, to_apply=%region_30.31 | all-reduce | flops 6144 | bytes 49152 | tf_op jit(solution)/shard_map/psum | solution.py:37
  (120 shorter events, 91.5 us)
Async XLA Ops:
  7.2 73.4 %copy-start = (bf16[2048,512]{1,0:T(8,128)(2,1)S(1)}, bf16[2048,512]{1,0:T(8,128)(2,1)}, u32[]{:S(2)}) copy-start(bf16[2048,512]{1,0:T(8,128)(2,1)} %param.11) | copy-start | bytes 6291460
  11.6 9.9 %copy-start.19 = (f32[3072]{0:T(1024)S(1)}, f32[3072]{0:T(1024)}, u32[]{:S(2)}) copy-start(f32[3072]{0:T(1024)} %param.13) | copy-start | bytes 36868
  11.6 9.9 %copy-start.20 = (f32[3072]{0:T(1024)S(1)}, f32[3072]{0:T(1024)}, u32[]{:S(2)}) copy-start(f32[3072]{0:T(1024)} %param.12) | copy-start | bytes 36868
  16.0 10.9 %all-to-all-start = ((f32[8,1,1024]{2,1,0:T(1,128)}), f32[8,1,1024]{2,1,0:T(1,128)S(1)}, u32[]{:S(2)}, u32[]{:S(2)}) async-start(f32[8,1,1024]{2,1,0:T(1,128)} %broadcast_in_dim.6), calls=%async_computation | async-start | bytes 65536 | tf_op jit(solution)/shard_map/all_to_all | solution.py:17
  46.5 2.1 copy-start.14
  46.5 3.0 copy-start.13
  60.0 2.1 copy-start.12
  60.0 2.9 copy-start.10
  62.1 1.8 copy-start.11
  86.4 9.4 %all-to-all-start.2 = ((f32[8,1,4096]{2,1,0:T(1,128)}), f32[8,1,4096]{2,1,0:T(1,128)S(1)}, u32[]{:S(2)}, u32[]{:S(2)}) async-start(f32[8,1,4096]{2,1,0:T(1,128)} %broadcast_in_dim.8), calls=%async_computation.2 | async-start | bytes 262144 | tf_op jit(solution)/shard_map/all_to_all | solution.py:17
  89.8 265.0 %reduce-scatter.2.cloned.1.call-start = ((), (), s32[]{:S(2)}) async-start(), calls=%async_computation.5 | async-start | bytes 20054016 | tf_op jit(solution)/shard_map/reduce_scatter | solution.py:167
  89.8 6.1 %slice-start.2 = ((f32[3072]{0:T(1024)}), f32[2048]{0:T(1024)S(1)}, s32[]{:S(2)}) async-start(f32[3072]{0:T(1024)} %param.13), calls=%async_computation.8 | async-start | bytes 16384 | tf_op jit(solution)/shard_map/slice | solution.py:128
  123.2 5.2 %copy-start.17 = (f32[588,512]{1,0:T(8,128)S(1)}, f32[588,512]{1,0:T(8,128)}, u32[]{:S(2)}) copy-start(f32[588,512]{1,0:T(8,128)} %get-tuple-element.62) | copy-start | bytes 3612676
  128.5 2.9 copy-start.15
  141.5 10.3 %slice-start = ((s8[5455872]{0:T(1024)(128)(4,1)}), s8[4194304]{0:T(1024)(128)(4,1)S(1)}, s32[]{:S(2)}) async-start(s8[5455872]{0:T(1024)(128)(4,1)} %bitcast.60), calls=%async_computation.6 | async-start | bytes 8388608
  143.7 8.1 %slice-start.1 = ((s8[5455872]{0:T(1024)(128)(4,1)}), s8[1261568]{0:T(1024)(128)(4,1)S(1)}, s32[]{:S(2)}) async-start(s8[5455872]{0:T(1024)(128)(4,1)} %bitcast.60), calls=%async_computation.7 | async-start | bytes 2523136
  151.8 6.3 %copy-start.16 = (bf16[588,2048]{1,0:T(8,128)(2,1)S(1)}, bf16[588,2048]{1,0:T(8,128)(2,1)}, u32[]{:S(2)}) copy-start(bf16[588,2048]{1,0:T(8,128)(2,1)} %copy-done.15) | copy-start | bytes 7225348
  151.8 6.3 %copy-start.18 = (f32[588,512]{1,0:T(8,128)S(1)}, f32[588,512]{1,0:T(8,128)}, u32[]{:S(2)}) copy-start(f32[588,512]{1,0:T(8,128)} %get-tuple-element.62) | copy-start | bytes 3612676
  208.6 1.6 copy-start.9
  210.5 1.4 copy-start.7
  212.2 1.4 copy-start.5
  233.0 1.7 copy-start.2
  357.9 62.7 %all-to-all-start.3 = ((f32[16,1088,32]{1,2,0:T(8,128)}), f32[16,1088,32]{1,2,0:T(8,128)}, u32[]{:S(2)}, u32[]{:S(2)}) async-start(f32[16,1088,32]{1,2,0:T(8,128)} %bitcast.50), calls=%async_computation.4 | async-start | bytes 4718592 | tf_op jit(solution)/shard_map/all_to_all | solution.py:48
  419.9 3.1 copy-start.1
  (4 other events, 5.3 us)
Sparse Core Ops, SparseCore 0:
  258.6 96.1 reduce-scatter.1
where the time goes:
time: 434 us; the launch traced here: 430 us
  local copies, waits for them, and re-layouts  118 us (27%)
  waiting for transfers between devices  103 us (24%)
  blocking collectives  90.4 us (21%)
  matrix products  47.9 us (11%)
  other arithmetic  40 us (9%)
  starting transfers between devices  15.7 us (4%)
  between operations  14.4 us (3%)
    reduce_scatter x1, waiting for transfers between devices, per_device(): lax.psum_scatter(local_grads, BNGROUP, scatter_dimension=0, tiled=True)  96.3 us
    psum x8, blocking collectives, by_axis(): value = lax.psum(value, axis)  82.6 us
    dot_general x6, matrix products, contract(): lax.dot_general(left, right, (((left_dim,), (right_dim,)), ((), ())), pre...  33.3 us
    slice x1, local copies, waits for them, and re-layouts, fold_back(): shaped[:, :, :, 3 * row_tap + col_tap, :]  32.4 us
    unnamed x62, local copies, waits for them, and re-layouts  18 us
    concatenate x9, local copies, waits for them, and re-layouts, unfold(): return jnp.concatenate(windows, axis=-1).reshape(-1, 9 * field.shape[3])  17.5 us
    concatenate x1, other arithmetic, per_device(): jnp.concatenate([contract(flat_in, grad_one, 0, 0), contract(patches, gra...  14.6 us
    dot_general x3, matrix products, matmul(): return jnp.dot(left, right, preferred_element_type=jnp.float32)  14.6 us
  transfers between devices with their start and end apart: 4, of which 3 were waited for; matrix products, arithmetic and copies ran while one was open for 5% of the time, Pallas kernels for 0%

commit v1 on v0

v1 whole, which is shorter than its diff:
```python
import functools

import jax
import jax.numpy as jnp
from jax import lax
from jax.experimental import pallas as pl
from jax.experimental.pallas import tpu as pltpu
from jax.sharding import PartitionSpec as P

MESH = pl.DeviceIdType.MESH
F32 = jnp.float32
BF16 = jnp.bfloat16

IMGS, SIDE, COLS = 12, 7, 8
WIDE, MID = 2048, 512
BAND = IMGS * COLS
ROWS = SIDE * BAND
REAL = IMGS * SIDE * SIDE
GROUP = 8
COUNT = float(REAL * GROUP)
IMAGES = 1536.0
EPS = 0.25
CH = 256
LANES = 2 * WIDE + 9 * MID
ZBLOCK = LANES // 4
OWN = 1152
VMEM_LIMIT = 67043328


def dot(left, right, dims=((1,), (0,))):
    return lax.dot_general(left, right, (dims, ((), ())), preferred_element_type=F32)


def sigmoid(value):
    return 0.5 * jnp.tanh(0.5 * value) + 0.5


def real_rows(value):
    rows, lanes = value.shape
    tiles = value.reshape(rows // 8, 8, lanes)
    column = lax.broadcasted_iota(jnp.int32, tiles.shape, 1)
    return jnp.where(column != 7, tiles, 0.0).reshape(rows, lanes)


def fold_rows(value):
    rows, lanes = value.shape
    return jnp.sum(value.reshape(rows // 8, 8, lanes), axis=0)


def total(folded):
    return jnp.sum(folded, axis=0, keepdims=True)


def lanes_at(j, size=CH):
    return pl.ds(pl.multiple_of(j * size, size), size)


def band_at(r):
    return pl.ds(pl.multiple_of(r * BAND, BAND), BAND)


def passes(
    x_hbm, cot_hbm, wr_hbm, ws_hbm, we_hbm, gain_ref, shift_ref,
    out_hbm, ing_hbm, wt_hbm, norm_ref,
    x, cot, wr, ws, we, pre1, taps, pre2, h2, pre3, up, g3, g2, back, g1, turned, stage, rows,
    s1, s2, s3, s4, s5, s6, load_sem, send_sem, recv_sem, stage_sem, out_sem,
):
    b = lax.axis_index("bngroup")

    def load(i, src, dst):
        copy = pltpu.make_async_copy(src, dst, load_sem.at[i])
        copy.start()
        return copy

    load_x = load(0, x_hbm, x)
    load_wr = load(1, wr_hbm, wr)
    load_ws = load(2, ws_hbm, ws)
    load_we = load(3, we_hbm, we)
    load_cot = load(4, cot_hbm, cot)

    barrier = pltpu.get_barrier_semaphore()
    for k in range(1, GROUP):
        pl.semaphore_signal(barrier, inc=1, device_id={"bngroup": (b + k) % GROUP}, device_id_type=MESH)

    zeros = jnp.zeros((BAND, 3 * MID), BF16)
    taps[0:BAND, :] = zeros
    taps[ROWS + BAND :, :] = zeros
    g2[0:BAND, :] = zeros
    g2[ROWS + BAND :, :] = zeros

    def share(e, slots):
        copies = []
        for k in range(1, GROUP):
            copy = pltpu.make_async_remote_copy(
                src_ref=slots.at[b],
                dst_ref=slots.at[b],
                send_sem=send_sem.at[e, k - 1],
                recv_sem=recv_sem.at[e, k - 1],
                device_id={"bngroup": (b + k) % GROUP},
                device_id_type=MESH,
            )
            copy.start()
            copies.append(copy)
        return copies

    def arrive(copies):
        for copy in copies:
            copy.wait()

    CEN, AMP, SHI, INV, SS, GS = range(6)
    OFF = {1: 0, 2: MID, 3: 2 * MID}
    SIZE = {1: MID, 2: MID, 3: WIDE}

    def put(row, norm, value):
        rows[row, :, OFF[norm] : OFF[norm] + SIZE[norm]] = value

    def get(row, norm, j):
        return rows[row, :, pl.ds(pl.multiple_of(OFF[norm] + j * CH, CH), CH)]

    def stats(pre, j, slots, channels):
        at = lanes_at(j)

        def add(r, acc):
            return acc + fold_rows(pre[band_at(r), at])

        mean = total(lax.fori_loop(0, SIDE, add, jnp.zeros((8, CH), F32))) / REAL

        def spread(r, acc):
            off = real_rows(pre[band_at(r), at] - mean)
            return acc + fold_rows(off * off)

        second = total(lax.fori_loop(0, SIDE, spread, jnp.zeros((8, CH), F32)))
        slots[b, :, at] = mean
        slots[b, :, pl.ds(pl.multiple_of(channels + j * CH, CH), CH)] = second

    def group_stats(slots, norm):
        c = SIZE[norm]
        mean = slots[0, :, 0:c]
        for i in range(1, GROUP):
            mean = mean + slots[i, :, 0:c]
        mean = mean / GROUP
        second = jnp.zeros((1, c), F32)
        for i in range(GROUP):
            off = slots[i, :, 0:c] - mean
            second = second + (slots[i, :, c : 2 * c] + REAL * (off * off))
        inverse = lax.rsqrt(second / COUNT + EPS)
        put(CEN, norm, mean)
        put(INV, norm, inverse)
        put(AMP, norm, gain_ref[:, OFF[norm] : OFF[norm] + c] * inverse)
        put(SHI, norm, shift_ref[:, OFF[norm] : OFF[norm] + c])

    def group_sums(slots, norm):
        c = SIZE[norm]
        sums = slots[0]
        for i in range(1, GROUP):
            sums = sums + slots[i]
        shift_sum, gain_sum = sums[:, 0:c], sums[:, c : 2 * c]
        inverse = rows[INV, :, OFF[norm] : OFF[norm] + c]
        norm_ref[:, OFF[norm] : OFF[norm] + c] = gain_sum
        norm_ref[:, 3072 + OFF[norm] : 3072 + OFF[norm] + c] = shift_sum
        put(SS, norm, shift_sum / COUNT)
        put(GS, norm, inverse * gain_sum / COUNT)

    load_x.wait()
    load_wr.wait()

    @pl.loop(0, MID // CH)
    def _(j):
        pre1[:, lanes_at(j)] = dot(x[...], wr[:, lanes_at(j)])
        stats(pre1, j, s1, MID)

    pl.semaphore_wait(barrier, GROUP - 1)
    arrive(share(0, s1))
    group_stats(s1, 1)

    @pl.loop(0, MID // CH)
    def _(j):
        cen, amp, shi = get(CEN, 1, j), get(AMP, 1, j), get(SHI, 1, j)

        @pl.loop(0, SIDE)
        def _(r):
            normed = (pre1[band_at(r), lanes_at(j)] - cen) * amp + shi
            hidden = real_rows(normed * sigmoid(normed))
            tiles = hidden.reshape(IMGS, 8, CH)
            to = pl.ds(pl.multiple_of((r + 1) * BAND, BAND), BAND)
            for tap, shifted in enumerate((pltpu.roll(tiles, 1, 1), tiles, pltpu.roll(tiles, 7, 1))):
                at = pl.ds(pl.multiple_of(tap * MID + j * CH, CH), CH)
                taps[to, at] = shifted.reshape(BAND, CH).astype(BF16)

    load_ws.wait()

    @pl.loop(0, MID // CH)
    def _(j):
        acc = dot(taps[0:ROWS, :], ws[0 : 3 * MID, lanes_at(j)])
        acc = acc + dot(taps[BAND : ROWS + BAND, :], ws[3 * MID : 6 * MID, lanes_at(j)])
        acc = acc + dot(taps[2 * BAND :, :], ws[6 * MID :, lanes_at(j)])
        pre2[:, lanes_at(j)] = real_rows(acc)
        stats(pre2, j, s2, MID)

    arrive(share(1, s2))
    group_stats(s2, 2)

    @pl.loop(0, MID // CH)
    def _(j):
        cen, amp, shi = get(CEN, 2, j), get(AMP, 2, j), get(SHI, 2, j)

        @pl.loop(0, SIDE)
        def _(r):
            normed = (pre2[band_at(r), lanes_at(j)] - cen) * amp + shi
            h2[band_at(r), lanes_at(j)] = real_rows(normed * sigmoid(normed)).astype(BF16)

    load_we.wait()

    @pl.loop(0, WIDE // CH)
    def _(j):
        pre3[:, lanes_at(j)] = dot(h2[...], we[lanes_at(j), :], ((1,), (1,)))
        stats(pre3, j, s3, WIDE)

    arrive(share(2, s3))
    group_stats(s3, 3)
    load_cot.wait()

    @pl.loop(0, WIDE // CH)
    def _(j):
        at = lanes_at(j)
        cen, amp, shi, inv = get(CEN, 3, j), get(AMP, 3, j), get(SHI, 3, j), get(INV, 3, j)

        def add(r, acc):
            band = band_at(r)
            centred = pre3[band, at] - cen
            summed = centred * amp + shi + x[band, at].astype(F32)
            sigma = sigmoid(summed)
            upstream = cot[band, at].astype(F32) * (sigma * (1.0 + summed * (1.0 - sigma)))
            cot[band, at] = (summed * sigma).astype(BF16)
            up[band, at] = upstream
            pre3[band, at] = centred
            return (acc[0] + fold_rows(upstream), acc[1] + fold_rows(upstream * centred))

        zero = jnp.zeros((8, CH), F32)
        shift_sum, gain_sum = lax.fori_loop(0, SIDE, add, (zero, zero))
        s4[b, :, at] = total(shift_sum)
        s4[b, :, pl.ds(pl.multiple_of(WIDE + j * CH, CH), CH)] = total(gain_sum) * inv

    sums = share(3, s4)
    write_out = pltpu.make_async_copy(cot, out_hbm, out_sem.at[0])
    write_out.start()
    arrive(sums)
    group_sums(s4, 3)

    @pl.loop(0, WIDE // CH)
    def _(j):
        at = lanes_at(j)
        amp, ss, gs = get(AMP, 3, j), get(SS, 3, j), get(GS, 3, j)

        @pl.loop(0, SIDE)
        def _(r):
            band = band_at(r)
            grad = amp * (up[band, at] - ss - pre3[band, at] * gs)
            g3[band, at] = real_rows(grad).astype(BF16)

    def slope_sums(pre, norm, j, slots):
        at = lanes_at(j)
        cen, amp, shi, inv = get(CEN, norm, j), get(AMP, norm, j), get(SHI, norm, j), get(INV, norm, j)

        def add(r, acc):
            band = band_at(r)
            centred = pre[band, at] - cen
            normed = centred * amp + shi
            sigma = sigmoid(normed)
            value = real_rows(back[band, at] * (sigma * (1.0 + normed * (1.0 - sigma))))
            back[band, at] = value
            return (acc[0] + fold_rows(value), acc[1] + fold_rows(value * centred))

        zero = jnp.zeros((8, CH), F32)
        shift_sum, gain_sum = lax.fori_loop(0, SIDE, add, (zero, zero))
        slots[b, :, at] = total(shift_sum)
        slots[b, :, pl.ds(pl.multiple_of(MID + j * CH, CH), CH)] = total(gain_sum) * inv

    def norm_back(pre, norm, j, r):
        at, band = lanes_at(j), band_at(r)
        cen, amp, ss, gs = get(CEN, norm, j), get(AMP, norm, j), get(SS, norm, j), get(GS, norm, j)
        return real_rows(amp * (back[band, at] - ss - (pre[band, at] - cen) * gs))

    @pl.loop(0, MID // CH)
    def _(j):
        back[:, lanes_at(j)] = dot(g3[...], we[:, lanes_at(j)])
        slope_sums(pre2, 2, j, s5)

    sums = share(4, s5)

    def weigh(first, count, place, right):
        @pl.loop(0, count)
        def _(q):
            slot = (first + q) % 2
            to = pl.ds(pl.multiple_of((place + q) * MID, MID), MID)
            copy = pltpu.make_async_copy(stage.at[slot], wt_hbm.at[:, :, :, to], stage_sem.at[slot])

            @pl.when(first + q >= 2)
            def _():
                copy.wait()

            for half in range(MID // CH):
                block = dot(turned[...], right(q, half)).reshape(16, 2, 16, CH)
                for core in range(2):
                    stage[slot, core, :, :, half * CH : (half + 1) * CH] = block[:, core]
            copy.start()

    turned[...] = h2[...].T
    weigh(0, 4, 13, lambda q, half: g3[:, pl.ds(pl.multiple_of(q * MID + half * CH, CH), CH)])

    arrive(sums)
    group_sums(s5, 2)

    @pl.loop(0, MID // CH)
    def _(j):
        @pl.loop(0, SIDE)
        def _(r):
            grad = norm_back(pre2, 2, j, r)
            tiles = grad.reshape(IMGS, 8, CH)
            to = pl.ds(pl.multiple_of((r + 1) * BAND, BAND), BAND)
            for tap, shifted in enumerate((pltpu.roll(tiles, 7, 1), tiles, pltpu.roll(tiles, 1, 1))):
                at = pl.ds(pl.multiple_of(tap * MID + j * CH, CH), CH)
                g2[to, at] = shifted.reshape(BAND, CH).astype(BF16)

    @pl.loop(0, MID // CH)
    def _(j):
        acc = None
        for row in range(3):
            for col in range(3):
                left = g2[(2 - row) * BAND : (2 - row) * BAND + ROWS, col * MID : (col + 1) * MID]
                at = pl.ds(pl.multiple_of((3 * row + col) * MID + j * CH, CH), CH)
                part = dot(left, ws[at, :], ((1,), (1,)))
                acc = part if acc is None else acc + part
        back[:, lanes_at(j)] = acc
        slope_sums(pre1, 1, j, s6)

    sums = share(5, s6)
    turned[...] = g2[BAND : ROWS + BAND, MID : 2 * MID].T
    weigh(
        4, 9, 4,
        lambda q, half: taps[
            pl.ds(pl.multiple_of((q // 3) * BAND, BAND), ROWS),
            pl.ds(pl.multiple_of((q % 3) * MID + half * CH, CH), CH),
        ],
    )
    arrive(sums)
    group_sums(s6, 1)

    @pl.loop(0, MID // CH)
    def _(j):
        @pl.loop(0, SIDE)
        def _(r):
            g1[band_at(r), lanes_at(j)] = norm_back(pre1, 1, j, r).astype(BF16)

    turned[...] = g1[...].T
    weigh(13, 4, 0, lambda q, half: x[:, pl.ds(pl.multiple_of(q * MID + half * CH, CH), CH)])

    @pl.loop(0, WIDE // CH)
    def _(j):
        at = lanes_at(j)
        g3[:, at] = (up[:, at] + dot(g1[...], wr[at, :], ((1,), (1,)))).astype(BF16)

    write_in = pltpu.make_async_copy(g3, ing_hbm, out_sem.at[1])
    write_in.start()
    for q in (15, 16):
        to = pl.ds(q * MID, MID)
        pltpu.make_async_copy(stage.at[q % 2], wt_hbm.at[:, :, :, to], stage_sem.at[q % 2]).wait()
    write_out.wait()
    write_in.wait()


def run_passes(x, cot, wr, ws, we, gain, shift):
    any_ = pl.BlockSpec(memory_space=pl.ANY)
    vmem = pl.BlockSpec(memory_space=pltpu.VMEM)
    v = pltpu.VMEM
    return pl.pallas_call(
        passes,
        out_shape=(
            jax.ShapeDtypeStruct((ROWS, WIDE), BF16),
            jax.ShapeDtypeStruct((ROWS, WIDE), BF16),
            jax.ShapeDtypeStruct((2, 16, 16, LANES), F32),
            jax.ShapeDtypeStruct((1, 6144), F32),
        ),
        in_specs=[any_] * 5 + [vmem] * 2,
        out_specs=(any_, any_, any_, vmem),
        scratch_shapes=[
            v((ROWS, WIDE), BF16),
            v((ROWS, WIDE), BF16),
            v((WIDE, MID), BF16),
            v((9 * MID, MID), BF16),
            v((WIDE, MID), BF16),
            v((ROWS, MID), F32),
            v((ROWS + 2 * BAND, 3 * MID), BF16),
            v((ROWS, MID), F32),
            v((ROWS, MID), BF16),
            v((ROWS, WIDE), F32),
            v((ROWS, WIDE), F32),
            v((ROWS, WIDE), BF16),
            v((ROWS + 2 * BAND, 3 * MID), BF16),
            v((ROWS, MID), F32),
            v((ROWS, MID), BF16),
            v((MID, ROWS), BF16),
            v((2, 2, 16, 16, MID), F32),
            v((6, 1, 3072), F32),
            v((GROUP, 1, 2 * MID), F32),
            v((GROUP, 1, 2 * MID), F32),
            v((GROUP, 1, 2 * WIDE), F32),
            v((GROUP, 1, 2 * WIDE), F32),
            v((GROUP, 1, 2 * MID), F32),
            v((GROUP, 1, 2 * MID), F32),
            pltpu.SemaphoreType.DMA((5,)),
            pltpu.SemaphoreType.DMA((6, GROUP - 1)),
            pltpu.SemaphoreType.DMA((6, GROUP - 1)),
            pltpu.SemaphoreType.DMA((2,)),
            pltpu.SemaphoreType.DMA((2,)),
        ],
        compiler_params=pltpu.CompilerParams(
            collective_id=0, has_side_effects=True, vmem_limit_bytes=VMEM_LIMIT
        ),
        cost_estimate=pl.CostEstimate(flops=18 * 10**9, bytes_accessed=4 * 10**7, transcendentals=10**7),
        name="passes",
    )(x, cot, wr, ws, we, gain, shift)


PIECES = ((0, 1024), (1024, 1024), (2048, 1024), (3072, 1280))
HALF = LANES // 2


def scatter(
    wt_hbm, norm_in, wg_ref, norm_out,
    own, other, first, second, third, fourth, last, ny, nx,
    core_send, core_recv, own_sem, send_sem, recv_sem, last_send, last_recv, norm_send, norm_recv,
):
    b, rep = lax.axis_index("bngroup"), lax.axis_index("rep")
    c = b % 2
    x, y = rep // 4, rep % 4

    def along(axis, k):
        if axis == "x":
            return {"rep": ((x + k) % 4) * 4 + y}
        return {"rep": x * 4 + (y + k) % 4}

    barrier = pltpu.get_barrier_semaphore()
    for k in range(1, GROUP):
        pl.semaphore_signal(barrier, inc=1, device_id={"bngroup": (b + k) % GROUP}, device_id_type=MESH)
    for axis in "xy":
        for k in range(1, 4):
            pl.semaphore_signal(barrier, inc=1, device_id=along(axis, k), device_id_type=MESH)

    spans = [pl.ds(color * HALF + at, size) for at, size in PIECES for color in range(2)]
    loads = []
    for i, span in enumerate(spans):
        copy = pltpu.make_async_copy(wt_hbm.at[c, :, :, :, span], own.at[:, :, :, span], own_sem.at[i])
        copy.start()
        loads.append(copy)
    pl.semaphore_wait(barrier, GROUP - 1 + 6)

    partner = {"bngroup": b + 1 - 2 * c}
    cores = []
    for i, span in enumerate(spans):
        copy = pltpu.make_async_remote_copy(
            src_ref=wt_hbm.at[1 - c, :, :, :, span],
            dst_ref=other.at[:, :, :, span],
            send_sem=core_send.at[i],
            recv_sem=core_recv.at[i],
            device_id=partner,
            device_id_type=MESH,
        )
        copy.start()
        cores.append(copy)

    def start(src, dst, device, piece, color, step, side):
        copy = pltpu.make_async_remote_copy(
            src_ref=src,
            dst_ref=dst,
            send_sem=send_sem.at[piece, color, step, side],
            recv_sem=recv_sem.at[piece, color, step, side],
            device_id=device,
            device_id_type=MESH,
        )
        copy.start()
        return copy

    def gather(step, axis, slots, mine, sem_send, sem_recv):
        copies = []
        for k in range(1, 4):
            copy = pltpu.make_async_remote_copy(
                src_ref=slots.at[mine],
                dst_ref=slots.at[mine],
                send_sem=sem_send.at[step, k - 1],
                recv_sem=sem_recv.at[step, k - 1],
                device_id=along(axis, k),
                device_id_type=MESH,
            )
            copy.start()
            copies.append(copy)
        return copies

    def sum_of(slots):
        return slots[0] + slots[1] + slots[2] + slots[3]

    ny[y] = norm_in[...]
    norm_copies = gather(0, "y", ny, y, norm_send, norm_recv)

    inflight = {}

    def stage_of(piece, step):
        at, size = PIECES[piece]
        half = size // 2
        for color in range(2):
            span = pl.ds(color * HALF + at, size)
            local = pl.ds(at, size)
            axes = "xy" if color == 0 else "yx"
            me = {"x": x, "y": y}
            outer, inner = me[axes[0]], me[axes[1]]

            def block(index, part=slice(None), span=span, color=color):
                if color == 0:
                    return own.at[index, part, :, span]
                return own.at[part, index, :, span]

            def inner_block(index, part_span, color=color, outer=outer):
                if color == 0:
                    return own.at[outer, index, :, part_span]
                return own.at[index, outer, :, part_span]

            def plus(k, base):
                return (base + k) % 4

            if step == 0:
                i = 2 * piece + color
                loads[i].wait()
                cores[i].wait()

                @pl.loop(0, 16)
                def _(n, span=span):
                    p, q = n // 4, n % 4
                    own[p, q, :, span] += other[p, q, :, span]

                opposite = plus(2, outer)
                inflight[piece, color, 0] = [
                    start(block(opposite, slice(0, 2)), first.at[color, 0, :, :, local], along(axes[0], 1), piece, color, 0, 0),
                    start(block(opposite, slice(2, 4)), first.at[color, 1, :, :, local], along(axes[0], 3), piece, color, 0, 1),
                ]
            elif step == 1:
                for copy in inflight[piece, color, 0]:
                    copy.wait()
                low = block(plus(1, outer), slice(0, 2))
                low[...] += first[color, 0, :, :, local]
                high = block(plus(3, outer), slice(2, 4))
                high[...] += first[color, 1, :, :, local]
                inflight[piece, color, 1] = [
                    start(block(plus(1, outer)), second.at[color, 0, :, :, local], along(axes[0], 1), piece, color, 1, 0),
                    start(block(plus(3, outer)), second.at[color, 1, :, :, local], along(axes[0], 3), piece, color, 1, 1),
                ]
            elif step == 2:
                for copy in inflight[piece, color, 1]:
                    copy.wait()
                mine = block(outer)
                mine[...] += second[color, 0, :, :, local] + second[color, 1, :, :, local]
                opposite = plus(2, inner)
                spans2 = [pl.ds(color * HALF + at, half), pl.ds(color * HALF + at + half, half)]
                local2 = pl.ds(at // 2, half)
                inflight[piece, color, 2] = [
                    start(inner_block(opposite, spans2[0]), third.at[color, 0, :, local2], along(axes[1], 1), piece, color, 2, 0),
                    start(inner_block(opposite, spans2[1]), third.at[color, 1, :, local2], along(axes[1], 3), piece, color, 2, 1),
                ]
            elif step == 3:
                for copy in inflight[piece, color, 2]:
                    copy.wait()
                spans2 = [pl.ds(color * HALF + at, half), pl.ds(color * HALF + at + half, half)]
                local2 = pl.ds(at // 2, half)
                low = inner_block(plus(1, inner), spans2[0])
                low[...] += third[color, 0, :, local2]
                high = inner_block(plus(3, inner), spans2[1])
                high[...] += third[color, 1, :, local2]
                inflight[piece, color, 3] = [
                    start(inner_block(plus(1, inner), span), fourth.at[color, 0, :, local], along(axes[1], 1), piece, color, 3, 0),
                    start(inner_block(plus(3, inner), span), fourth.at[color, 1, :, local], along(axes[1], 3), piece, color, 3, 1),
                ]
            else:
                for copy in inflight[piece, color, 3]:
                    copy.wait()
                mine = inner_block(inner, span)
                mine[...] += fourth[color, 0, :, local] + fourth[color, 1, :, local]

    for t in range(len(PIECES) + 4):
        for step in reversed(range(5)):
            if 0 <= t - step < len(PIECES):
                stage_of(t - step, step)

    def owned(device):
        return pl.ds(pl.multiple_of((device // 2) * ZBLOCK + (device % 2) * 1024, 128), OWN)

    finals = []
    for k in range(1, GROUP):
        peer = (b + k) % GROUP
        copy = pltpu.make_async_remote_copy(
            src_ref=own.at[x, y, :, owned(peer)],
            dst_ref=last.at[b],
            send_sem=last_send.at[k - 1],
            recv_sem=last_recv.at[k - 1],
            device_id={"bngroup": peer},
            device_id_type=MESH,
        )
        copy.start()
        finals.append(copy)
    last[b] = own[x, y, :, owned(b)]

    for copy in norm_copies:
        copy.wait()
    nx[x] = sum_of(ny)
    norm_copies = gather(1, "x", nx, x, norm_send, norm_recv)

    for copy in finals:
        copy.wait()
    parts = []
    for core in range(2):
        parts.append(last[core] + last[2 + core] + last[4 + core] + last[6 + core])
    whole = jnp.concatenate(parts, axis=0) * (1.0 / IMAGES)
    turned = pltpu.roll(whole, OWN - 64, 1)
    wg_ref[...] = jnp.where(c == 1, turned, whole)[:, : LANES // 8]
    for copy in norm_copies:
        copy.wait()
    norm_out[...] = sum_of(nx) * (1.0 / IMAGES)


def run_scatter(wt, norm):
    any_ = pl.BlockSpec(memory_space=pl.ANY)
    vmem = pl.BlockSpec(memory_space=pltpu.VMEM)
    v = pltpu.VMEM
    dma = pltpu.SemaphoreType.DMA
    n = len(PIECES)
    return pl.pallas_call(
        scatter,
        out_shape=(
            jax.ShapeDtypeStruct((32, LANES // 8), F32),
            jax.ShapeDtypeStruct((1, 6144), F32),
        ),
        in_specs=[any_, vmem],
        out_specs=(vmem, vmem),
        scratch_shapes=[
            v((4, 4, 16, LANES), F32),
            v((4, 4, 16, LANES), F32),
            v((2, 2, 2, 16, HALF), F32),
            v((2, 2, 4, 16, HALF), F32),
            v((2, 2, 16, HALF // 2), F32),
            v((2, 2, 16, HALF), F32),
            v((GROUP, 16, OWN), F32),
            v((4, 1, 6144), F32),
            v((4, 1, 6144), F32),
            dma((2 * n,)),
            dma((2 * n,)),
            dma((2 * n,)),
            dma((n, 2, 4, 2)),
            dma((n, 2, 4, 2)),
            dma((GROUP - 1,)),
            dma((GROUP - 1,)),
            dma((2, 3)),
            dma((2, 3)),
        ],
        compiler_params=pltpu.CompilerParams(
            collective_id=1, has_side_effects=True, vmem_limit_bytes=VMEM_LIMIT
        ),
        cost_estimate=pl.CostEstimate(flops=10**7, bytes_accessed=2 * 10**7, transcendentals=0),
        name="scatter",
    )(wt.reshape(2, 4, 4, 16, LANES), norm)


def to_rows(images):
    padded = jnp.pad(images, ((0, 0), (0, 0), (0, 1), (0, 0)))
    return padded.transpose(1, 0, 2, 3).reshape(ROWS, WIDE)


def from_rows(rows):
    return rows.reshape(SIDE, IMGS, COLS, WIDE)[:, :, :SIDE].transpose(1, 0, 2, 3)


def per_device(images, cotangent, w_reduce, w_spatial, w_expand, norm_gain, norm_shift):
    output, in_grad, wt, norms = run_passes(
        to_rows(images), to_rows(cotangent), w_reduce, w_spatial, w_expand,
        norm_gain.reshape(1, -1), norm_shift.reshape(1, -1),
    )
    grads, norm_grads = run_scatter(wt, norms)
    return (from_rows(output), from_rows(in_grad), grads.T, norm_grads.reshape(2, -1))


def solution(mesh):
    both = P(("bngroup", "rep"), None, None, None)
    return jax.shard_map(
        per_device,
        mesh=mesh,
        in_specs=(both, both, P(), P(), P(), P(), P()),
        out_specs=(both, both, P("bngroup", "rep"), P()),
        check_vma=False,
    )
```

time: 434 us -> 158 us (0.36)
  Pallas kernels: 0 us -> 140 us
  local copies, waits for them, and re-layouts: 118 us -> 14 us
  waiting for transfers between devices: 103 us -> 0 us
  blocking collectives: 90.4 us -> 0 us
  matrix products: 47.9 us -> 0 us
  other arithmetic: 40 us -> 1.44 us
  starting transfers between devices: 15.7 us -> 0 us
  between operations: 14.4 us -> 0.68 us
    pallas_call x0 -> x2, Pallas kernels: none -> 140 us  [the longest x1 73.2 us: run_scatter(): pl.pallas_call(scatter, out_shape=(jax.ShapeDtypeStruct((32, LANES // 8),...]
    reduce_scatter x1 -> x0, waiting for transfers between devices: 96.3 us -> none  [per_device(): lax.psum_scatter(local_grads, BNGROUP, scatter_dimension=0, tiled=True)]
    psum x8 -> x0, blocking collectives: 82.6 us -> none  [by_axis(): value = lax.psum(value, axis)]
    dot_general x9 -> x0, matrix products: 47.9 us -> none  [the longest x6 33.3 us: contract(): lax.dot_general(left, right, (((left_dim,), (right_dim,)), ((), ())), pre...]
    slice x6 -> x0, local copies, waits for them, and re-layouts: 38.5 us -> none  [the longest x1 32.4 us: fold_back(): shaped[:, :, :, 3 * row_tap + col_tap, :]]
    reshape x6 -> x1, local copies, waits for them, and re-layouts: 30 us -> 0.62 us  [per_device(): norm_grads.reshape(2, -1)]
    concatenate x9 -> x0, local copies, waits for them, and re-layouts: 17.5 us -> none  [unfold(): return jnp.concatenate(windows, axis=-1).reshape(-1, 9 * field.shape[3])]
    unnamed x62 -> x5, local copies, waits for them, and re-layouts: 18 us -> 1.71 us
  transfers between devices with their start and end apart: 4 -> 0, of which waited for: 3 -> 0; matrix products, arithmetic and copies ran while one was open for 5% -> 0% of each run, Pallas kernels for 0% -> 0%
where the time goes in v1:
time: 158 us; the launch traced here: 156 us
  Pallas kernels  140 us (89%)
  local copies, waits for them, and re-layouts  14 us (9%)
    pallas_call x1, Pallas kernels, run_scatter(): pl.pallas_call(scatter, out_shape=(jax.ShapeDtypeStruct((32, LANES // 8),...  73.2 us
    pallas_call x1, Pallas kernels, run_passes(): pl.pallas_call(passes, out_shape=(jax.ShapeDtypeStruct((ROWS, WIDE), BF16...  67.1 us
    transpose x4, local copies, waits for them, and re-layouts, to_rows(): return padded.transpose(1, 0, 2, 3).reshape(ROWS, WIDE)  6.59 us
    transpose x1, local copies, waits for them, and re-layouts, from_rows(): rows.reshape(SIDE, IMGS, COLS, WIDE)[:, :, :SIDE].transpose(1, 0, 2, 3)  4.58 us

profile of v1, /device:TPU:0, one launch (start us, length us, event | category | flops | bytes accessed | tf_op | source)
XLA Modules:
  0.0 156.4 jit_solution(2070223786659209544)
XLA Ops:
  0.6 2.4 %pad_bitcast_fusion.1 = bf16[7,12,8,2048]{3,2,0,1:T(8,128)(2,1)S(1)} fusion(bf16[12,7,7,2048]{3,2,1,0:T(8,128)(2,1)} %param.7), kind=kLoop, calls=%fused_computation.3 | loop fusion | bytes 5160960 | tf_op jit(solution)/shard_map/transpose | solution.py:672
  3.0 0.0 copy-start
  3.0 1.7 %copy.11 = bf16[7,12,8,2048]{3,2,1,0:T(8,128)(2,1)} copy(bf16[7,12,8,2048]{3,2,0,1:T(8,128)(2,1)S(1)} %pad_bitcast_fusion.1) | data formatting | bytes 5505024 | tf_op jit(solution)/shard_map/transpose | solution.py:672
  4.8 1.0 copy-done
  5.8 0.7 pad_bitcast_fusion
  6.6 1.7 %copy.12 = bf16[7,12,8,2048]{3,2,1,0:T(8,128)(2,1)} copy(bf16[7,12,8,2048]{3,2,0,1:T(8,128)(2,1)S(1)} %pad_bitcast_fusion) | data formatting | bytes 5505024 | tf_op jit(solution)/shard_map/transpose | solution.py:672
  8.3 67.1 %passes.1 = (bf16[672,2048]{1,0:T(8,128)(2,1)}, bf16[672,2048]{1,0:T(8,128)(2,1)}, f32[2,16,16,8704]{3,2,1,0:T(8,128)}, f32[1,6144]{1,0:T(1,128)}) custom-call(bf16[672,2048]{1,0:T(8,128)(2,1)} %bitcast.19, bf16[672,2048]{1,0:T(8,128)(2,1)} %bitcast.20, bf16[2048,512]{1,0:T(8,128)(2,1)} %wr_hbm.1, bf16[4608,512]{1,0:T(8,128)(2,1)} %ws_hbm.1, ...), custom_call_target="tpu_custom_call" | custom-call | flops 17999998976 | bytes 40000000 | tf_op jit(solution)/shard_map/passes/pallas_call | solution.py:376
  75.4 73.2 %scatter.1 = (f32[32,1088]{1,0:T(8,128)}, f32[1,6144]{1,0:T(1,128)}) custom-call(f32[2,4,4,16,8704]{4,3,2,1,0:T(8,128)} %bitcast.16, f32[1,6144]{1,0:T(1,128)} %get-tuple-element.13.norm_in), custom_call_target="tpu_custom_call" | custom-call | flops 10000000 | bytes 20000000 | tf_op jit(solution)/shard_map/scatter/pallas_call | solution.py:634
  148.6 0.5 broadcast.7
  149.1 1.4 reduce.3
  150.6 0.6 reshape.39
  151.2 0.0 copy-start.1
  151.2 4.6 %copy_bitcast_fusion = (bf16[12,7,7,2048]{3,2,1,0:T(8,128)(2,1)}, bf16[12,7,7,2048]{3,2,1,0:T(8,128)(2,1)}) fusion(bf16[7,12,8,2048]{3,2,1,0:T(8,128)(2,1)} %bitcast.17, bf16[7,12,8,2048]{3,2,1,0:T(8,128)(2,1)} %bitcast.18), kind=kLoop, calls=%fused_computation | loop fusion | bytes 10321920 | tf_op jit(solution)/shard_map/transpose | solution.py:676
  155.8 0.0 copy-done.1
  155.8 0.7 copy.20
Async XLA Ops:
  3.0 2.8 %copy-start = (bf16[12,7,7,2048]{3,2,1,0:T(8,128)(2,1)S(1)}, bf16[12,7,7,2048]{3,2,1,0:T(8,128)(2,1)}, u32[]{:S(2)}) copy-start(bf16[12,7,7,2048]{3,2,1,0:T(8,128)(2,1)} %param.8) | copy-start | bytes 7225348
  151.2 4.6 %copy-start.1 = (f32[32,1088]{1,0:T(8,128)S(1)}, f32[32,1088]{1,0:T(8,128)}, u32[]{:S(2)}) copy-start(f32[32,1088]{1,0:T(8,128)} %get-tuple-element.14) | copy-start | bytes 417796

commit v2 on v1

v2 whole, which is shorter than its diff:
```python
import jax
import jax.numpy as jnp
from jax import lax
from jax.experimental import pallas as pl
from jax.experimental.pallas import tpu as pltpu
from jax.sharding import PartitionSpec as P

MESH = pl.DeviceIdType.MESH
F32 = jnp.float32
BF16 = jnp.bfloat16

IMGS, SIDE, COLS = 12, 7, 8
WIDE, MID = 2048, 512
BAND = IMGS * COLS
ROWS = SIDE * BAND
REAL = IMGS * SIDE * SIDE
GROUP = 8
COUNT = float(REAL * GROUP)
IMAGES = 1536.0
EPS = 0.25
CH = 256
LANES = 2 * WIDE + 9 * MID
ZBLOCK = LANES // 4
OWN = 1152
VMEM_LIMIT = 67043328
SLOTS = 4

PIECES = {
    "expand": (6656, 2048, 0, 4),
    "low": (2048, 1536, 4, 3),
    "mid": (3584, 1536, 7, 3),
    "high": (5120, 1536, 10, 3),
    "reduce": (0, 2048, 13, 4),
}
SHARE = {}
_ab, _c = 0, 0
for _name, (_lane, _size, _, _) in PIECES.items():
    _n = (_size - 512) // 2
    SHARE[_name] = (_n, _ab, _c)
    _ab, _c = _ab + _n, _c + 128
AB_LANES, C_LANES = _ab, _c


def dot(left, right, dims=((1,), (0,))):
    return lax.dot_general(left, right, (dims, ((), ())), preferred_element_type=F32)


def sigmoid(value):
    return 0.5 * jnp.tanh(0.5 * value) + 0.5


def real_rows(value):
    rows, lanes = value.shape
    tiles = value.reshape(rows // 8, 8, lanes)
    column = lax.broadcasted_iota(jnp.int32, tiles.shape, 1)
    return jnp.where(column != 7, tiles, 0.0).reshape(rows, lanes)


def fold_rows(value):
    rows, lanes = value.shape
    return jnp.sum(value.reshape(rows // 8, 8, lanes), axis=0)


def total(folded):
    return jnp.sum(folded, axis=0, keepdims=True)


def lanes_at(j, size=CH):
    return pl.ds(pl.multiple_of(j * size, size), size)


def band_at(r):
    return pl.ds(pl.multiple_of(r * BAND, BAND), BAND)


def block(
    x_hbm, cot_hbm, wr_hbm, ws_hbm, we_hbm, gain_ref, shift_ref,
    out_hbm, ing_hbm, wg_ref, norm_out,
    x, cot, wa, ws, pre1, taps, pre2, h2, pre3, up, g3, g2, back, turned, stage, rows,
    s1, s2, s3, s4, s5, s6, norm, own, other, ab1, ab2, ab3, ab4, c1, c2, c3, c4, last, ny, nx,
    load_sem, send_sem, recv_sem, out_sem, core_send, core_recv,
    ab_send, ab_recv, cz_send, cz_recv, cd_send, cd_recv, last_send, last_recv, norm_send, norm_recv,
):
    b, rep = lax.axis_index("bngroup"), lax.axis_index("rep")
    z, c = b // 2, b % 2
    xx, yy = rep // 4, rep % 4

    def along(axis, k):
        if axis == "x":
            return {"rep": ((xx + k) % 4) * 4 + yy}
        if axis == "y":
            return {"rep": xx * 4 + (yy + k) % 4}
        return {"bngroup": (b + 2 * k) % GROUP}

    def load(i, src, dst):
        copy = pltpu.make_async_copy(src, dst, load_sem.at[i])
        copy.start()
        return copy

    load_x = load(0, x_hbm, x)
    load_wr = load(1, wr_hbm, wa)
    load_ws = load(2, ws_hbm, ws)
    load_cot = load(4, cot_hbm, cot)

    barrier = pltpu.get_barrier_semaphore()
    for k in range(1, GROUP):
        pl.semaphore_signal(barrier, inc=1, device_id={"bngroup": (b + k) % GROUP}, device_id_type=MESH)
    for axis in "xy":
        for k in range(1, 4):
            pl.semaphore_signal(barrier, inc=1, device_id=along(axis, k), device_id_type=MESH)

    zeros = jnp.zeros((BAND, 3 * MID), BF16)
    taps[0:BAND, :] = zeros
    taps[ROWS + BAND :, :] = zeros
    g2[0:BAND, :] = zeros
    g2[ROWS + BAND :, :] = zeros

    def share(e, slots):
        copies = []
        for k in range(1, GROUP):
            copy = pltpu.make_async_remote_copy(
                src_ref=slots.at[b],
                dst_ref=slots.at[b],
                send_sem=send_sem.at[e, k - 1],
                recv_sem=recv_sem.at[e, k - 1],
                device_id={"bngroup": (b + k) % GROUP},
                device_id_type=MESH,
            )
            copy.start()
            copies.append(copy)
        return copies

    def arrive(copies):
        for copy in copies:
            copy.wait()

    CEN, AMP, SHI, INV, SS, GS = range(6)
    OFF = {1: 0, 2: MID, 3: 2 * MID}
    SIZE = {1: MID, 2: MID, 3: WIDE}

    def put(row, which, value):
        rows[row, :, OFF[which] : OFF[which] + SIZE[which]] = value

    def get(row, which, j):
        return rows[row, :, pl.ds(pl.multiple_of(OFF[which] + j * CH, CH), CH)]

    def stats(pre, j, slots, channels):
        at = lanes_at(j)

        def add(r, acc):
            return acc + fold_rows(pre[band_at(r), at])

        mean = total(lax.fori_loop(0, SIDE, add, jnp.zeros((8, CH), F32))) / REAL

        def spread(r, acc):
            off = real_rows(pre[band_at(r), at] - mean)
            return acc + fold_rows(off * off)

        second = total(lax.fori_loop(0, SIDE, spread, jnp.zeros((8, CH), F32)))
        slots[b, :, at] = mean
        slots[b, :, pl.ds(pl.multiple_of(channels + j * CH, CH), CH)] = second

    def group_stats(slots, which):
        c = SIZE[which]
        mean = slots[0, :, 0:c]
        for i in range(1, GROUP):
            mean = mean + slots[i, :, 0:c]
        mean = mean / GROUP
        second = jnp.zeros((1, c), F32)
        for i in range(GROUP):
            off = slots[i, :, 0:c] - mean
            second = second + (slots[i, :, c : 2 * c] + REAL * (off * off))
        inverse = lax.rsqrt(second / COUNT + EPS)
        put(CEN, which, mean)
        put(INV, which, inverse)
        put(AMP, which, gain_ref[:, OFF[which] : OFF[which] + c] * inverse)
        put(SHI, which, shift_ref[:, OFF[which] : OFF[which] + c])

    def group_sums(slots, which):
        c = SIZE[which]
        sums = slots[0]
        for i in range(1, GROUP):
            sums = sums + slots[i]
        shift_sum, gain_sum = sums[:, 0:c], sums[:, c : 2 * c]
        inverse = rows[INV, :, OFF[which] : OFF[which] + c]
        norm[0:1, OFF[which] : OFF[which] + c] = gain_sum
        norm[1:2, OFF[which] : OFF[which] + c] = shift_sum
        put(SS, which, shift_sum / COUNT)
        put(GS, which, inverse * gain_sum / COUNT)

    load_x.wait()
    load_wr.wait()

    @pl.loop(0, MID // CH)
    def _(j):
        pre1[:, lanes_at(j)] = dot(x[...], wa[:, lanes_at(j)])
        stats(pre1, j, s1, MID)

    load_we = load(3, we_hbm, wa)
    pl.semaphore_wait(barrier, GROUP - 1 + 6)
    arrive(share(0, s1))
    group_stats(s1, 1)

    @pl.loop(0, MID // CH)
    def _(j):
        cen, amp, shi = get(CEN, 1, j), get(AMP, 1, j), get(SHI, 1, j)

        @pl.loop(0, SIDE)
        def _(r):
            normed = (pre1[band_at(r), lanes_at(j)] - cen) * amp + shi
            hidden = real_rows(normed * sigmoid(normed))
            tiles = hidden.reshape(IMGS, 8, CH)
            to = pl.ds(pl.multiple_of((r + 1) * BAND, BAND), BAND)
            for tap, shifted in enumerate((pltpu.roll(tiles, 1, 1), tiles, pltpu.roll(tiles, 7, 1))):
                at = pl.ds(pl.multiple_of(tap * MID + j * CH, CH), CH)
                taps[to, at] = shifted.reshape(BAND, CH).astype(BF16)

    load_ws.wait()

    @pl.loop(0, MID // CH)
    def _(j):
        acc = dot(taps[0:ROWS, :], ws[0 : 3 * MID, lanes_at(j)])
        acc = acc + dot(taps[BAND : ROWS + BAND, :], ws[3 * MID : 6 * MID, lanes_at(j)])
        acc = acc + dot(taps[2 * BAND :, :], ws[6 * MID :, lanes_at(j)])
        pre2[:, lanes_at(j)] = real_rows(acc)
        stats(pre2, j, s2, MID)

    arrive(share(1, s2))
    group_stats(s2, 2)

    @pl.loop(0, MID // CH)
    def _(j):
        cen, amp, shi = get(CEN, 2, j), get(AMP, 2, j), get(SHI, 2, j)

        @pl.loop(0, SIDE)
        def _(r):
            normed = (pre2[band_at(r), lanes_at(j)] - cen) * amp + shi
            h2[band_at(r), lanes_at(j)] = real_rows(normed * sigmoid(normed)).astype(BF16)

    load_we.wait()

    @pl.loop(0, WIDE // CH)
    def _(j):
        pre3[:, lanes_at(j)] = dot(h2[...], wa[lanes_at(j), :], ((1,), (1,)))
        stats(pre3, j, s3, WIDE)

    arrive(share(2, s3))
    group_stats(s3, 3)
    load_cot.wait()

    @pl.loop(0, WIDE // CH)
    def _(j):
        at = lanes_at(j)
        cen, amp, shi, inv = get(CEN, 3, j), get(AMP, 3, j), get(SHI, 3, j), get(INV, 3, j)

        def add(r, acc):
            band = band_at(r)
            centred = pre3[band, at] - cen
            summed = centred * amp + shi + x[band, at].astype(F32)
            sigma = sigmoid(summed)
            upstream = cot[band, at].astype(F32) * (sigma * (1.0 + summed * (1.0 - sigma)))
            cot[band, at] = (summed * sigma).astype(BF16)
            up[band, at] = upstream
            pre3[band, at] = centred
            return (acc[0] + fold_rows(upstream), acc[1] + fold_rows(upstream * centred))

        zero = jnp.zeros((8, CH), F32)
        shift_sum, gain_sum = lax.fori_loop(0, SIDE, add, (zero, zero))
        s4[b, :, at] = total(shift_sum)
        s4[b, :, pl.ds(pl.multiple_of(WIDE + j * CH, CH), CH)] = total(gain_sum) * inv

    sums = share(3, s4)
    write_out = pltpu.make_async_copy(cot, out_hbm, out_sem.at[0])
    write_out.start()
    arrive(sums)
    group_sums(s4, 3)

    @pl.loop(0, WIDE // CH)
    def _(j):
        at = lanes_at(j)
        amp, ss, gs = get(AMP, 3, j), get(SS, 3, j), get(GS, 3, j)

        @pl.loop(0, SIDE)
        def _(r):
            band = band_at(r)
            grad = amp * (up[band, at] - ss - pre3[band, at] * gs)
            g3[band, at] = real_rows(grad).astype(BF16)

    def slope_sums(pre, which, j, slots):
        at = lanes_at(j)
        cen, amp, shi, inv = get(CEN, which, j), get(AMP, which, j), get(SHI, which, j), get(INV, which, j)

        def add(r, acc):
            band = band_at(r)
            centred = pre[band, at] - cen
            normed = centred * amp + shi
            sigma = sigmoid(normed)
            value = real_rows(back[band, at] * (sigma * (1.0 + normed * (1.0 - sigma))))
            back[band, at] = value
            return (acc[0] + fold_rows(value), acc[1] + fold_rows(value * centred))

        zero = jnp.zeros((8, CH), F32)
        shift_sum, gain_sum = lax.fori_loop(0, SIDE, add, (zero, zero))
        slots[b, :, at] = total(shift_sum)
        slots[b, :, pl.ds(pl.multiple_of(MID + j * CH, CH), CH)] = total(gain_sum) * inv

    def norm_back(pre, which, j, r):
        at, band = lanes_at(j), band_at(r)
        cen, amp, ss, gs = get(CEN, which, j), get(AMP, which, j), get(SS, which, j), get(GS, which, j)
        return real_rows(amp * (back[band, at] - ss - (pre[band, at] - cen) * gs))

    @pl.loop(0, MID // CH)
    def _(j):
        back[:, lanes_at(j)] = dot(g3[...], wa[:, lanes_at(j)])
        slope_sums(pre2, 2, j, s5)

    sums = share(4, s5)
    load_wr = load(5, wr_hbm, wa)

    def turn(value):
        halves = value.T.reshape(16, 2, 16, ROWS)
        for half in range(2):
            turned[(half + c + 1) % 2] = halves[:, half].reshape(MID // 2, ROWS)

    def landing(piece, at):
        if piece == "expand":
            return pre3.at[0:256, at]
        if piece == "reduce":
            return pre3.at[256:512, at]
        return other.at[:, at]

    def to_partner(piece, i):
        lane, size, chunk, _ = PIECES[piece]
        start = lane - 2048 if piece in ("low", "mid", "high") else 0
        at = pl.ds(pl.multiple_of(start + i * MID, MID), MID)
        return pltpu.make_async_remote_copy(
            src_ref=stage.at[(chunk + i) % SLOTS],
            dst_ref=landing(piece, at),
            send_sem=core_send.at[chunk + i],
            recv_sem=core_recv.at[chunk + i],
            device_id={"bngroup": b + 1 - 2 * c},
            device_id_type=MESH,
        )

    def slot_free(n):
        pltpu.make_async_remote_copy(
            src_ref=stage.at[n % SLOTS],
            dst_ref=other.at[:, 0:MID],
            send_sem=core_send.at[n],
            recv_sem=core_recv.at[n],
            device_id={"bngroup": b + 1 - 2 * c},
            device_id_type=MESH,
        ).wait_send()

    def weigh(piece, right):
        lane, size, chunk, count = PIECES[piece]

        @pl.loop(0, count)
        def _(i):
            slot = (chunk + i) % SLOTS
            if chunk >= SLOTS:
                slot_free(chunk + i - SLOTS)
            for half in range(MID // CH):
                product = dot(turned[...].reshape(MID, ROWS), right(i, half))
                stage[slot, :, half * CH : (half + 1) * CH] = product[: MID // 2]
                at = pl.ds(pl.multiple_of(lane + i * MID + half * CH, CH), CH)
                own[:, :, :, at] = product[MID // 2 :].reshape(4, 4, 16, CH)
            if piece != "expand":
                to_partner(piece, i).start()

    flying = {}

    def send(src, dst, device, sems):
        copy = pltpu.make_async_remote_copy(
            src_ref=src, dst_ref=dst, send_sem=sems[0], recv_sem=sems[1],
            device_id=device, device_id_type=MESH,
        )
        copy.start()
        return copy

    def plus(k, base):
        return (base + k) % 4

    names = list(PIECES)

    def step(piece, n):
        lane, size, chunk, count = PIECES[piece]
        width, ab_at, c_at = SHARE[piece]
        p = names.index(piece)
        half = width // 2
        if n == 0:
            for i in range(count):
                to_partner(piece, i).wait_recv()
            start = lane - 2048 if piece in ("low", "mid", "high") else 0
            landed = landing(piece, pl.ds(start, size))

            @pl.loop(0, 16)
            def _(k):
                own[k // 4, k % 4, :, lane : lane + size] += landed[pl.ds(pl.multiple_of(k * 16, 16), 16), :]

        else:
            for copy in flying.pop((piece, n - 1)):
                copy.wait()
        copies = []
        for color in range(2):
            span = pl.ds(lane + color * width, width)
            local = pl.ds(ab_at, width)
            axes = "xy" if color == 0 else "yx"
            outer, inner = (xx, yy) if color == 0 else (yy, xx)
            parts = [pl.ds(lane + color * width + k * half, half) for k in range(2)]
            local_part = pl.ds(ab_at // 2, half)
            sems = [(ab_send.at[p, color, n, side], ab_recv.at[p, color, n, side]) for side in range(2)] if n < 4 else None

            def outer_block(index, part=slice(None), color=color, span=span):
                return own.at[index, part, :, span] if color == 0 else own.at[part, index, :, span]

            def inner_block(index, part, color=color, outer=outer):
                return own.at[outer, index, :, part] if color == 0 else own.at[index, outer, :, part]

            if n == 0:
                far = plus(2, outer)
                copies.append(send(outer_block(far, slice(0, 2)), ab1.at[color, 0, :, :, local], along(axes[0], 1), sems[0]))
                copies.append(send(outer_block(far, slice(2, 4)), ab1.at[color, 1, :, :, local], along(axes[0], 3), sems[1]))
            elif n == 1:
                low = outer_block(plus(1, outer), slice(0, 2))
                low[...] += ab1[color, 0, :, :, local]
                high = outer_block(plus(3, outer), slice(2, 4))
                high[...] += ab1[color, 1, :, :, local]
                copies.append(send(outer_block(plus(1, outer)), ab2.at[color, 0, :, :, local], along(axes[0], 1), sems[0]))
                copies.append(send(outer_block(plus(3, outer)), ab2.at[color, 1, :, :, local], along(axes[0], 3), sems[1]))
            elif n == 2:
                mine = outer_block(outer)
                mine[...] += ab2[color, 0, :, :, local] + ab2[color, 1, :, :, local]
                far = plus(2, inner)
                copies.append(send(inner_block(far, parts[0]), ab3.at[color, 0, :, local_part], along(axes[1], 1), sems[0]))
                copies.append(send(inner_block(far, parts[1]), ab3.at[color, 1, :, local_part], along(axes[1], 3), sems[1]))
            elif n == 3:
                low = inner_block(plus(1, inner), parts[0])
                low[...] += ab3[color, 0, :, local_part]
                high = inner_block(plus(3, inner), parts[1])
                high[...] += ab3[color, 1, :, local_part]
                copies.append(send(inner_block(plus(1, inner), span), ab4.at[color, 0, :, local], along(axes[1], 1), sems[0]))
                copies.append(send(inner_block(plus(3, inner), span), ab4.at[color, 1, :, local], along(axes[1], 3), sems[1]))
            else:
                mine = inner_block(inner, span)
                mine[...] += ab4[color, 0, :, local] + ab4[color, 1, :, local]

        base = lane + 2 * width
        local = pl.ds(c_at, 128)

        def tile(index):
            return pl.ds(pl.multiple_of(base + 128 * index, 128), 128)

        if n < 2:
            sems = [(cz_send.at[p, n, side], cz_recv.at[p, n, side]) for side in range(2)]
        elif n < 4:
            sems = [(cd_send.at[p, n - 2, k], cd_recv.at[p, n - 2, k]) for k in range(3)]
        if n == 0:
            far = tile(plus(2, z))
            copies.append(send(own.at[0:2, :, :, far], c1.at[0, :, :, :, local], along("z", 1), sems[0]))
            copies.append(send(own.at[2:4, :, :, far], c1.at[1, :, :, :, local], along("z", 3), sems[1]))
        elif n == 1:
            up_one, down_one = tile(plus(1, z)), tile(plus(3, z))
            own[0:2, :, :, up_one] += c1[0, :, :, :, local]
            own[2:4, :, :, down_one] += c1[1, :, :, :, local]
            copies.append(send(own.at[:, :, :, up_one], c2.at[0, :, :, :, local], along("z", 1), sems[0]))
            copies.append(send(own.at[:, :, :, down_one], c2.at[1, :, :, :, local], along("z", 3), sems[1]))
        elif n == 2:
            own[:, :, :, tile(z)] += c2[0, :, :, :, local] + c2[1, :, :, :, local]
            for k in range(1, 4):
                copies.append(send(own.at[plus(k, xx), :, :, tile(z)], c3.at[k - 1, :, :, local], along("x", k), sems[k - 1]))
        elif n == 3:
            own[xx, :, :, tile(z)] += c3[0, :, :, local] + c3[1, :, :, local] + c3[2, :, :, local]
            for k in range(1, 4):
                copies.append(send(own.at[xx, plus(k, yy), :, tile(z)], c4.at[k - 1, :, local], along("y", k), sems[k - 1]))
        else:
            mine = own[xx, yy, :, tile(z)] + c4[0, :, local] + c4[1, :, local] + c4[2, :, local]
            own[xx, yy, :, base : base + 512] = jnp.zeros((16, 512), F32)
            own[xx, yy, :, tile(z)] = mine
        if n < 4:
            flying[piece, n] = copies

    def owned(device):
        return pl.ds(pl.multiple_of((device // 2) * ZBLOCK + (device % 2) * 1024, 128), OWN)

    def to_owner(t):
        return pltpu.make_async_remote_copy(
            src_ref=own.at[xx, yy, :, owned(t)],
            dst_ref=last.at[b],
            send_sem=last_send.at[t],
            recv_sem=last_recv.at[b],
            device_id={"bngroup": t},
            device_id_type=MESH,
        )

    def from_member(t):
        return pltpu.make_async_remote_copy(
            src_ref=own.at[xx, yy, :, owned(b)],
            dst_ref=last.at[t],
            send_sem=last_send.at[t],
            recv_sem=last_recv.at[t],
            device_id={"bngroup": t},
            device_id_type=MESH,
        )

    def to_owners(targets):
        for t in targets:

            @pl.when(b != t)
            def _(t=t):
                to_owner(t).start()

    def gather(n, axis, slots, mine):
        return [
            send(slots.at[mine], slots.at[mine], along(axis, k), (norm_send.at[n, k - 1], norm_recv.at[n, k - 1]))
            for k in range(1, 4)
        ]

    def sum_of(slots):
        return slots[0] + slots[1] + slots[2] + slots[3]

    turn(h2[...])
    weigh("expand", lambda i, half: g3[:, pl.ds(pl.multiple_of(i * MID + half * CH, CH), CH)])

    arrive(sums)
    for i in range(4):
        to_partner("expand", i).start()
    group_sums(s5, 2)

    @pl.loop(0, MID // CH)
    def _(j):
        @pl.loop(0, SIDE)
        def _(r):
            grad = norm_back(pre2, 2, j, r)
            tiles = grad.reshape(IMGS, 8, CH)
            to = pl.ds(pl.multiple_of((r + 1) * BAND, BAND), BAND)
            for tap, shifted in enumerate((pltpu.roll(tiles, 7, 1), tiles, pltpu.roll(tiles, 1, 1))):
                at = pl.ds(pl.multiple_of(tap * MID + j * CH, CH), CH)
                g2[to, at] = shifted.reshape(BAND, CH).astype(BF16)

    step("expand", 0)

    for j in range(MID // CH):
        acc = None
        for row in range(3):
            for col in range(3):
                left = g2[(2 - row) * BAND : (2 - row) * BAND + ROWS, col * MID : (col + 1) * MID]
                at = pl.ds((3 * row + col) * MID + j * CH, CH)
                part = dot(left, ws[at, :], ((1,), (1,)))
                acc = part if acc is None else acc + part
        back[:, j * CH : (j + 1) * CH] = acc
        slope_sums(pre1, 1, j, s6)
        if j == 0:
            step("expand", 1)

    sums = share(5, s6)
    turn(g2[BAND : ROWS + BAND, MID : 2 * MID])

    def tap_row(row):
        return lambda i, half: taps[
            row * BAND : row * BAND + ROWS,
            pl.ds(pl.multiple_of(i * MID + half * CH, CH), CH),
        ]

    weigh("low", tap_row(0))
    step("expand", 2)
    step("low", 0)
    weigh("mid", tap_row(1))
    step("expand", 3)
    step("low", 1)
    step("mid", 0)
    weigh("high", tap_row(2))
    arrive(sums)
    group_sums(s6, 1)
    ny[yy] = norm[...]
    norm_copies = gather(0, "y", ny, yy)

    @pl.loop(0, MID // CH)
    def _(j):
        @pl.loop(0, SIDE)
        def _(r):
            h2[band_at(r), lanes_at(j)] = norm_back(pre1, 1, j, r).astype(BF16)

    step("expand", 4)
    step("low", 2)
    step("mid", 1)
    step("high", 0)
    turn(h2[...])
    weigh("reduce", lambda i, half: x[:, pl.ds(pl.multiple_of(i * MID + half * CH, CH), CH)])
    step("low", 3)
    step("mid", 2)
    step("high", 1)
    step("reduce", 0)

    load_wr.wait()

    @pl.loop(0, WIDE // CH)
    def _(j):
        at = lanes_at(j)
        g3[:, at] = (up[:, at] + dot(h2[...], wa[at, :], ((1,), (1,)))).astype(BF16)

    write_in = pltpu.make_async_copy(g3, ing_hbm, out_sem.at[1])
    write_in.start()

    step("low", 4)
    step("mid", 3)
    step("high", 2)
    step("reduce", 1)
    step("mid", 4)
    step("high", 3)
    for copy in norm_copies:
        copy.wait()
    nx[xx] = sum_of(ny)
    norm_copies = gather(1, "x", nx, xx)
    step("reduce", 2)
    step("high", 4)
    to_owners(range(2, GROUP))
    step("reduce", 3)
    step("reduce", 4)
    to_owners(range(2))
    last[b] = own[xx, yy, :, owned(b)]

    for copy in norm_copies:
        copy.wait()
    norm_out[...] = sum_of(nx) * (1.0 / IMAGES)
    write_out.wait()
    write_in.wait()
    for n in range(13, 17):
        slot_free(n)
    for t in range(GROUP):

        @pl.when(b != t)
        def _(t=t):
            to_owner(t).wait_send()
            from_member(t).wait_recv()

    parts = []
    for core in range(2):
        parts.append(last[core] + last[2 + core] + last[4 + core] + last[6 + core])
    whole = jnp.concatenate(parts, axis=0) * (1.0 / IMAGES)
    moved = pltpu.roll(whole, OWN - 64, 1)
    wg_ref[...] = jnp.where(c == 1, moved, whole)[:, : LANES // 8]


def run_block(x, cot, wr, ws, we, gain, shift):
    any_ = pl.BlockSpec(memory_space=pl.ANY)
    vmem = pl.BlockSpec(memory_space=pltpu.VMEM)
    v = pltpu.VMEM
    dma = pltpu.SemaphoreType.DMA
    pieces = len(PIECES)
    return pl.pallas_call(
        block,
        out_shape=(
            jax.ShapeDtypeStruct((ROWS, WIDE), BF16),
            jax.ShapeDtypeStruct((ROWS, WIDE), BF16),
            jax.ShapeDtypeStruct((32, LANES // 8), F32),
            jax.ShapeDtypeStruct((2, 3072), F32),
        ),
        in_specs=[any_] * 5 + [vmem] * 2,
        out_specs=(any_, any_, vmem, vmem),
        scratch_shapes=[
            v((ROWS, WIDE), BF16),
            v((ROWS, WIDE), BF16),
            v((WIDE, MID), BF16),
            v((9 * MID, MID), BF16),
            v((ROWS, MID), F32),
            v((ROWS + 2 * BAND, 3 * MID), BF16),
            v((ROWS, MID), F32),
            v((ROWS, MID), BF16),
            v((ROWS, WIDE), F32),
            v((ROWS, WIDE), F32),
            v((ROWS, WIDE), BF16),
            v((ROWS + 2 * BAND, 3 * MID), BF16),
            v((ROWS, MID), F32),
            v((2, MID // 2, ROWS), BF16),
            v((SLOTS, MID // 2, MID), F32),
            v((6, 1, 3072), F32),
            v((GROUP, 1, 2 * MID), F32),
            v((GROUP, 1, 2 * MID), F32),
            v((GROUP, 1, 2 * WIDE), F32),
            v((GROUP, 1, 2 * WIDE), F32),
            v((GROUP, 1, 2 * MID), F32),
            v((GROUP, 1, 2 * MID), F32),
            v((2, 3072), F32),
            v((4, 4, 16, LANES), F32),
            v((MID // 2, 9 * MID), F32),
            v((2, 2, 2, 16, AB_LANES), F32),
            v((2, 2, 4, 16, AB_LANES), F32),
            v((2, 2, 16, AB_LANES // 2), F32),
            v((2, 2, 16, AB_LANES), F32),
            v((2, 2, 4, 16, C_LANES), F32),
            v((2, 4, 4, 16, C_LANES), F32),
            v((3, 4, 16, C_LANES), F32),
            v((3, 16, C_LANES), F32),
            v((GROUP, 16, OWN), F32),
            v((4, 2, 3072), F32),
            v((4, 2, 3072), F32),
            dma((6,)),
            dma((6, GROUP - 1)),
            dma((6, GROUP - 1)),
            dma((2,)),
            dma((17,)),
            dma((17,)),
            dma((pieces, 2, 4, 2)),
            dma((pieces, 2, 4, 2)),
            dma((pieces, 2, 2)),
            dma((pieces, 2, 2)),
            dma((pieces, 2, 3)),
            dma((pieces, 2, 3)),
            dma((GROUP,)),
            dma((GROUP,)),
            dma((2, 3)),
            dma((2, 3)),
        ],
        compiler_params=pltpu.CompilerParams(
            collective_id=0, has_side_effects=True, vmem_limit_bytes=VMEM_LIMIT
        ),
        cost_estimate=pl.CostEstimate(flops=18 * 10**9, bytes_accessed=4 * 10**7, transcendentals=10**7),
        name="block",
    )(x, cot, wr, ws, we, gain, shift)


def to_rows(images):
    padded = jnp.pad(images, ((0, 0), (0, 0), (0, 1), (0, 0)))
    return padded.transpose(1, 0, 2, 3).reshape(ROWS, WIDE)


def from_rows(rows):
    return rows.reshape(SIDE, IMGS, COLS, WIDE)[:, :, :SIDE].transpose(1, 0, 2, 3)


def per_device(images, cotangent, w_reduce, w_spatial, w_expand, norm_gain, norm_shift):
    output, in_grad, grads, norm_grads = run_block(
        to_rows(images), to_rows(cotangent), w_reduce, w_spatial, w_expand,
        norm_gain.reshape(1, -1), norm_shift.reshape(1, -1),
    )
    return (from_rows(output), from_rows(in_grad), grads.T, norm_grads)


def solution(mesh):
    both = P(("bngroup", "rep"), None, None, None)
    return jax.shard_map(
        per_device,
        mesh=mesh,
        in_specs=(both, both, P(), P(), P(), P(), P()),
        out_specs=(both, both, P("bngroup", "rep"), P()),
        check_vma=False,
    )
```

time: 158 us -> 133 us (0.84)
  Pallas kernels: 140 us -> 117 us
    pallas_call x2 -> x1, Pallas kernels: 140 us -> 117 us  [run_block(): pl.pallas_call(block, out_shape=(jax.ShapeDtypeStruct((ROWS, WIDE), BF16)...]
where the time goes in v2:
time: 133 us; the launch traced here: 131 us
  Pallas kernels  117 us (88%)
  local copies, waits for them, and re-layouts  13.5 us (10%)
    pallas_call x1, Pallas kernels, run_block(): pl.pallas_call(block, out_shape=(jax.ShapeDtypeStruct((ROWS, WIDE), BF16)...  117 us
    transpose x4, local copies, waits for them, and re-layouts, to_rows(): return padded.transpose(1, 0, 2, 3).reshape(ROWS, WIDE)  6.59 us
    transpose x1, local copies, waits for them, and re-layouts, from_rows(): rows.reshape(SIDE, IMGS, COLS, WIDE)[:, :, :SIDE].transpose(1, 0, 2, 3)  4.61 us

profile of v2, /device:TPU:0, one launch (start us, length us, event | category | flops | bytes accessed | tf_op | source)
XLA Modules:
  0.0 131.2 jit_solution(12705276319242243967)
XLA Ops:
  0.6 2.4 %pad_bitcast_fusion.1 = bf16[7,12,8,2048]{3,2,0,1:T(8,128)(2,1)S(1)} fusion(bf16[12,7,7,2048]{3,2,1,0:T(8,128)(2,1)} %param.7), kind=kLoop, calls=%fused_computation.3 | loop fusion | bytes 5160960 | tf_op jit(solution)/shard_map/transpose | solution.py:725
  3.0 0.0 copy-start
  3.0 1.7 %copy.11 = bf16[7,12,8,2048]{3,2,1,0:T(8,128)(2,1)} copy(bf16[7,12,8,2048]{3,2,0,1:T(8,128)(2,1)S(1)} %pad_bitcast_fusion.1) | data formatting | bytes 5505024 | tf_op jit(solution)/shard_map/transpose | solution.py:725
  4.8 1.0 copy-done
  5.8 0.7 pad_bitcast_fusion
  6.6 1.7 %copy.12 = bf16[7,12,8,2048]{3,2,1,0:T(8,128)(2,1)} copy(bf16[7,12,8,2048]{3,2,0,1:T(8,128)(2,1)S(1)} %pad_bitcast_fusion) | data formatting | bytes 5505024 | tf_op jit(solution)/shard_map/transpose | solution.py:725
  8.3 117.0 %block.1 = (bf16[672,2048]{1,0:T(8,128)(2,1)}, bf16[672,2048]{1,0:T(8,128)(2,1)}, f32[32,1088]{1,0:T(8,128)}, f32[2,3072]{1,0:T(2,128)}) custom-call(bf16[672,2048]{1,0:T(8,128)(2,1)} %bitcast.15, bf16[672,2048]{1,0:T(8,128)(2,1)} %bitcast.18, bf16[2048,512]{1,0:T(8,128)(2,1)} %wr_hbm.1, bf16[4608,512]{1,0:T(8,128)(2,1)} %ws_hbm.1, ...), custom_call_target="tpu_custom_call" | custom-call | flops 17999998976 | bytes 40000000 | tf_op jit(solution)/shard_map/block/pallas_call | solution.py:651
  125.3 0.0 copy-start.1
  125.3 0.0 copy-start.2
  125.3 4.6 %copy_bitcast_fusion = (bf16[12,7,7,2048]{3,2,1,0:T(8,128)(2,1)}, bf16[12,7,7,2048]{3,2,1,0:T(8,128)(2,1)}) fusion(bf16[7,12,8,2048]{3,2,1,0:T(8,128)(2,1)} %bitcast.16, bf16[7,12,8,2048]{3,2,1,0:T(8,128)(2,1)} %bitcast.17), kind=kLoop, calls=%fused_computation | loop fusion | bytes 10321920 | tf_op jit(solution)/shard_map/transpose | solution.py:729
  129.9 0.0 copy-done.1
  129.9 0.7 copy.21
  130.6 0.0 copy-done.2
  130.6 0.6 copy.22
Async XLA Ops:
  3.0 2.8 %copy-start = (bf16[12,7,7,2048]{3,2,1,0:T(8,128)(2,1)S(1)}, bf16[12,7,7,2048]{3,2,1,0:T(8,128)(2,1)}, u32[]{:S(2)}) copy-start(bf16[12,7,7,2048]{3,2,1,0:T(8,128)(2,1)} %param.8) | copy-start | bytes 7225348
  125.3 4.6 %copy-start.1 = (f32[32,1088]{1,0:T(8,128)S(1)}, f32[32,1088]{1,0:T(8,128)}, u32[]{:S(2)}) copy-start(f32[32,1088]{1,0:T(8,128)} %get-tuple-element.10) | copy-start | bytes 417796
  125.3 5.3 %copy-start.2 = (f32[2,3072]{1,0:T(2,128)S(1)}, f32[2,3072]{1,0:T(2,128)}, u32[]{:S(2)}) copy-start(f32[2,3072]{1,0:T(2,128)} %get-tuple-element.21) | copy-start | bytes 73732

commit v3 on v2

--- a/solution.py
+++ b/solution.py
@@ -30,8 +30,10 @@
     "low": (2048, 1536, 4, 3),
     "mid": (3584, 1536, 7, 3),
     "high": (5120, 1536, 10, 3),
-    "reduce": (0, 2048, 13, 4),
+    "upper": (1024, 1024, 13, 2),
+    "first": (0, 1024, 15, 2),
 }
+LANDING = {"expand": 0, "low": 0, "mid": 1536, "high": 3072, "upper": 1024, "first": 0}
 SHARE = {}
 _ab, _c = 0, 0
 for _name, (_lane, _size, _, _) in PIECES.items():
@@ -79,7 +81,7 @@
     x, cot, wa, ws, pre1, taps, pre2, h2, pre3, up, g3, g2, back, turned, stage, rows,
     s1, s2, s3, s4, s5, s6, norm, own, other, ab1, ab2, ab3, ab4, c1, c2, c3, c4, last, ny, nx,
     load_sem, send_sem, recv_sem, out_sem, core_send, core_recv,
-    ab_send, ab_recv, cz_send, cz_recv, cd_send, cd_recv, last_send, last_recv, norm_send, norm_recv,
+    ab_send, ab_recv, cz_send, cz_recv, cd_send, cd_recv, last_send, last_recv, norm_send, norm_recv, ready,
 ):
     b, rep = lax.axis_index("bngroup"), lax.axis_index("rep")
     z, c = b // 2, b % 2
@@ -99,8 +101,6 @@
 
     load_x = load(0, x_hbm, x)
     load_wr = load(1, wr_hbm, wa)
-    load_ws = load(2, ws_hbm, ws)
-    load_cot = load(4, cot_hbm, cot)
 
     barrier = pltpu.get_barrier_semaphore()
     for k in range(1, GROUP):
@@ -190,6 +190,8 @@
 
     load_x.wait()
     load_wr.wait()
+    load_ws = load(2, ws_hbm, ws)
+    load_cot = load(4, cot_hbm, cot)
 
     @pl.loop(0, MID // CH)
     def _(j):
@@ -269,54 +271,6 @@
         s4[b, :, at] = total(shift_sum)
         s4[b, :, pl.ds(pl.multiple_of(WIDE + j * CH, CH), CH)] = total(gain_sum) * inv
 
-    sums = share(3, s4)
-    write_out = pltpu.make_async_copy(cot, out_hbm, out_sem.at[0])
-    write_out.start()
-    arrive(sums)
-    group_sums(s4, 3)
-
-    @pl.loop(0, WIDE // CH)
-    def _(j):
-        at = lanes_at(j)
-        amp, ss, gs = get(AMP, 3, j), get(SS, 3, j), get(GS, 3, j)
-
-        @pl.loop(0, SIDE)
-        def _(r):
-            band = band_at(r)
-            grad = amp * (up[band, at] - ss - pre3[band, at] * gs)
-            g3[band, at] = real_rows(grad).astype(BF16)
-
-    def slope_sums(pre, which, j, slots):
-        at = lanes_at(j)
-        cen, amp, shi, inv = get(CEN, which, j), get(AMP, which, j), get(SHI, which, j), get(INV, which, j)
-
-        def add(r, acc):
-            band = band_at(r)
-            centred = pre[band, at] - cen
-            normed = centred * amp + shi
-            sigma = sigmoid(normed)
-            value = real_rows(back[band, at] * (sigma * (1.0 + normed * (1.0 - sigma))))
-            back[band, at] = value
-            return (acc[0] + fold_rows(value), acc[1] + fold_rows(value * centred))
-
-        zero = jnp.zeros((8, CH), F32)
-        shift_sum, gain_sum = lax.fori_loop(0, SIDE, add, (zero, zero))
-        slots[b, :, at] = total(shift_sum)
-        slots[b, :, pl.ds(pl.multiple_of(MID + j * CH, CH), CH)] = total(gain_sum) * inv
-
-    def norm_back(pre, which, j, r):
-        at, band = lanes_at(j), band_at(r)
-        cen, amp, ss, gs = get(CEN, which, j), get(AMP, which, j), get(SS, which, j), get(GS, which, j)
-        return real_rows(amp * (back[band, at] - ss - (pre[band, at] - cen) * gs))
-
-    @pl.loop(0, MID // CH)
-    def _(j):
-        back[:, lanes_at(j)] = dot(g3[...], wa[:, lanes_at(j)])
-        slope_sums(pre2, 2, j, s5)
-
-    sums = share(4, s5)
-    load_wr = load(5, wr_hbm, wa)
-
     def turn(value):
         halves = value.T.reshape(16, 2, 16, ROWS)
         for half in range(2):
@@ -325,13 +279,13 @@
     def landing(piece, at):
         if piece == "expand":
             return pre3.at[0:256, at]
-        if piece == "reduce":
+        if piece in ("upper", "first"):
             return pre3.at[256:512, at]
         return other.at[:, at]
 
     def to_partner(piece, i):
         lane, size, chunk, _ = PIECES[piece]
-        start = lane - 2048 if piece in ("low", "mid", "high") else 0
+        start = LANDING[piece]
         at = pl.ds(pl.multiple_of(start + i * MID, MID), MID)
         return pltpu.make_async_remote_copy(
             src_ref=stage.at[(chunk + i) % SLOTS],
@@ -365,8 +319,7 @@
                 stage[slot, :, half * CH : (half + 1) * CH] = product[: MID // 2]
                 at = pl.ds(pl.multiple_of(lane + i * MID + half * CH, CH), CH)
                 own[:, :, :, at] = product[MID // 2 :].reshape(4, 4, 16, CH)
-            if piece != "expand":
-                to_partner(piece, i).start()
+            to_partner(piece, i).start()
 
     flying = {}
 
@@ -391,7 +344,7 @@
         if n == 0:
             for i in range(count):
                 to_partner(piece, i).wait_recv()
-            start = lane - 2048 if piece in ("low", "mid", "high") else 0
+            start = LANDING[piece]
             landed = landing(piece, pl.ds(start, size))
 
             @pl.loop(0, 16)
@@ -451,6 +404,8 @@
         def tile(index):
             return pl.ds(pl.multiple_of(base + 128 * index, 128), 128)
 
+        first_axis = "x" if p % 2 == 0 else "y"
+        second_axis = "y" if p % 2 == 0 else "x"
         if n < 2:
             sems = [(cz_send.at[p, n, side], cz_recv.at[p, n, side]) for side in range(2)]
         elif n < 4:
@@ -468,11 +423,14 @@
         elif n == 2:
             own[:, :, :, tile(z)] += c2[0, :, :, :, local] + c2[1, :, :, :, local]
             for k in range(1, 4):
-                copies.append(send(own.at[plus(k, xx), :, :, tile(z)], c3.at[k - 1, :, :, local], along("x", k), sems[k - 1]))
+                block_of = own.at[plus(k, xx), :, :, tile(z)] if p % 2 == 0 else own.at[:, plus(k, yy), :, tile(z)]
+                copies.append(send(block_of, c3.at[k - 1, :, :, local], along(first_axis, k), sems[k - 1]))
         elif n == 3:
-            own[xx, :, :, tile(z)] += c3[0, :, :, local] + c3[1, :, :, local] + c3[2, :, :, local]
+            mine = own.at[xx, :, :, tile(z)] if p % 2 == 0 else own.at[:, yy, :, tile(z)]
+            mine[...] += c3[0, :, :, local] + c3[1, :, :, local] + c3[2, :, :, local]
             for k in range(1, 4):
-                copies.append(send(own.at[xx, plus(k, yy), :, tile(z)], c4.at[k - 1, :, local], along("y", k), sems[k - 1]))
+                block_of = own.at[xx, plus(k, yy), :, tile(z)] if p % 2 == 0 else own.at[plus(k, xx), yy, :, tile(z)]
+                copies.append(send(block_of, c4.at[k - 1, :, local], along(second_axis, k), sems[k - 1]))
         else:
             mine = own[xx, yy, :, tile(z)] + c4[0, :, local] + c4[1, :, local] + c4[2, :, local]
             own[xx, yy, :, base : base + 512] = jnp.zeros((16, 512), F32)
@@ -519,12 +477,60 @@
     def sum_of(slots):
         return slots[0] + slots[1] + slots[2] + slots[3]
 
+    sums = share(3, s4)
+    write_out = pltpu.make_async_copy(cot, out_hbm, out_sem.at[0])
+    write_out.start()
     turn(h2[...])
+    arrive(sums)
+    group_sums(s4, 3)
+
+    @pl.loop(0, WIDE // CH)
+    def _(j):
+        at = lanes_at(j)
+        amp, ss, gs = get(AMP, 3, j), get(SS, 3, j), get(GS, 3, j)
+
+        @pl.loop(0, SIDE)
+        def _(r):
+            band = band_at(r)
+            grad = amp * (up[band, at] - ss - pre3[band, at] * gs)
+            g3[band, at] = real_rows(grad).astype(BF16)
+
+    def slope_sums(pre, which, j, slots):
+        at = lanes_at(j)
+        cen, amp, shi, inv = get(CEN, which, j), get(AMP, which, j), get(SHI, which, j), get(INV, which, j)
+
+        def add(r, acc):
+            band = band_at(r)
+            centred = pre[band, at] - cen
+            normed = centred * amp + shi
+            sigma = sigmoid(normed)
+            value = real_rows(back[band, at] * (sigma * (1.0 + normed * (1.0 - sigma))))
+            back[band, at] = value
+            return (acc[0] + fold_rows(value), acc[1] + fold_rows(value * centred))
+
+        zero = jnp.zeros((8, CH), F32)
+        shift_sum, gain_sum = lax.fori_loop(0, SIDE, add, (zero, zero))
+        slots[b, :, at] = total(shift_sum)
+        slots[b, :, pl.ds(pl.multiple_of(MID + j * CH, CH), CH)] = total(gain_sum) * inv
+
+    def norm_back(pre, which, j, r):
+        at, band = lanes_at(j), band_at(r)
+        cen, amp, ss, gs = get(CEN, which, j), get(AMP, which, j), get(SS, which, j), get(GS, which, j)
+        return real_rows(amp * (back[band, at] - ss - (pre[band, at] - cen) * gs))
+
+    pl.semaphore_signal(ready, inc=1, device_id={"bngroup": b + 1 - 2 * c}, device_id_type=MESH)
+    pl.semaphore_wait(ready, 1)
     weigh("expand", lambda i, half: g3[:, pl.ds(pl.multiple_of(i * MID + half * CH, CH), CH)])
-
+    @pl.loop(0, MID // CH)
+    def _(j):
+        back[:, lanes_at(j)] = dot(g3[...], wa[:, lanes_at(j)])
+        slope_sums(pre2, 2, j, s5)
+
+    sums = share(4, s5)
+    load_wr = load(5, wr_hbm, wa)
+
+    step("expand", 0)
     arrive(sums)
-    for i in range(4):
-        to_partner("expand", i).start()
     group_sums(s5, 2)
 
     @pl.loop(0, MID // CH)
@@ -538,9 +544,13 @@
                 at = pl.ds(pl.multiple_of(tap * MID + j * CH, CH), CH)
                 g2[to, at] = shifted.reshape(BAND, CH).astype(BF16)
 
-    step("expand", 0)
-
-    for j in range(MID // CH):
+    def tap_row(row):
+        return lambda i, half: taps[
+            row * BAND : row * BAND + ROWS,
+            pl.ds(pl.multiple_of(i * MID + half * CH, CH), CH),
+        ]
+
+    def back_one(j):
         acc = None
         for row in range(3):
             for col in range(3):
@@ -550,26 +560,24 @@
                 acc = part if acc is None else acc + part
         back[:, j * CH : (j + 1) * CH] = acc
         slope_sums(pre1, 1, j, s6)
-        if j == 0:
-            step("expand", 1)
-
+
+    turn(g2[BAND : ROWS + BAND, MID : 2 * MID])
+    weigh("low", tap_row(0))
+    weigh("mid", tap_row(1))
+    step("low", 0)
+    step("expand", 1)
+    weigh("high", tap_row(2))
+    step("mid", 0)
+    back_one(0)
+    step("high", 0)
+    step("low", 1)
+    step("expand", 2)
+    back_one(1)
     sums = share(5, s6)
-    turn(g2[BAND : ROWS + BAND, MID : 2 * MID])
-
-    def tap_row(row):
-        return lambda i, half: taps[
-            row * BAND : row * BAND + ROWS,
-            pl.ds(pl.multiple_of(i * MID + half * CH, CH), CH),
-        ]
-
-    weigh("low", tap_row(0))
-    step("expand", 2)
-    step("low", 0)
-    weigh("mid", tap_row(1))
+    step("mid", 1)
     step("expand", 3)
-    step("low", 1)
-    step("mid", 0)
-    weigh("high", tap_row(2))
+    step("high", 1)
+    step("low", 2)
     arrive(sums)
     group_sums(s6, 1)
     ny[yy] = norm[...]
@@ -581,16 +589,15 @@
         def _(r):
             h2[band_at(r), lanes_at(j)] = norm_back(pre1, 1, j, r).astype(BF16)
 
+    turn(h2[...])
+    weigh("upper", lambda i, half: x[:, pl.ds(pl.multiple_of(1024 + i * MID + half * CH, CH), CH)])
+    weigh("first", lambda i, half: x[:, pl.ds(pl.multiple_of(i * MID + half * CH, CH), CH)])
+    step("upper", 0)
+    step("mid", 2)
+    step("first", 0)
+    step("high", 2)
+    step("low", 3)
     step("expand", 4)
-    step("low", 2)
-    step("mid", 1)
-    step("high", 0)
-    turn(h2[...])
-    weigh("reduce", lambda i, half: x[:, pl.ds(pl.multiple_of(i * MID + half * CH, CH), CH)])
-    step("low", 3)
-    step("mid", 2)
-    step("high", 1)
-    step("reduce", 0)
 
     load_wr.wait()
 
@@ -602,22 +609,26 @@
     write_in = pltpu.make_async_copy(g3, ing_hbm, out_sem.at[1])
     write_in.start()
 
+    step("upper", 1)
+    step("mid", 3)
+    step("first", 1)
+    step("high", 3)
     step("low", 4)
-    step("mid", 3)
-    step("high", 2)
-    step("reduce", 1)
-    step("mid", 4)
-    step("high", 3)
     for copy in norm_copies:
         copy.wait()
     nx[xx] = sum_of(ny)
     norm_copies = gather(1, "x", nx, xx)
-    step("reduce", 2)
+    step("upper", 2)
+    step("mid", 4)
+    step("first", 2)
     step("high", 4)
-    to_owners(range(2, GROUP))
-    step("reduce", 3)
-    step("reduce", 4)
-    to_owners(range(2))
+    to_owners(range(2, 8))
+    step("upper", 3)
+    step("first", 3)
+    step("upper", 4)
+    to_owners(range(1, 2))
+    step("first", 4)
+    to_owners(range(0, 1))
     last[b] = own[xx, yy, :, owned(b)]
 
     for copy in norm_copies:
@@ -711,6 +722,7 @@
             dma((GROUP,)),
             dma((2, 3)),
             dma((2, 3)),
+            pltpu.SemaphoreType.REGULAR,
         ],
         compiler_params=pltpu.CompilerParams(
             collective_id=0, has_side_effects=True, vmem_limit_bytes=VMEM_LIMIT

time: 133 us -> 121 us (0.910); the launches traced: 131 us -> 121 us
  Pallas kernels: 117 us -> 107 us
    pallas_call x1, Pallas kernels: 117 us -> 107 us  [run_block(): pl.pallas_call(block, out_shape=(jax.ShapeDtypeStruct((ROWS, WIDE), BF16)...]
where the time goes in v3:
time: 121 us
  Pallas kernels  107 us (88%)
  local copies, waits for them, and re-layouts  13.5 us (11%)
    pallas_call x1, Pallas kernels, run_block(): pl.pallas_call(block, out_shape=(jax.ShapeDtypeStruct((ROWS, WIDE), BF16)...  107 us
    transpose x4, local copies, waits for them, and re-layouts, to_rows(): return padded.transpose(1, 0, 2, 3).reshape(ROWS, WIDE)  6.59 us
    transpose x1, local copies, waits for them, and re-layouts, from_rows(): rows.reshape(SIDE, IMGS, COLS, WIDE)[:, :, :SIDE].transpose(1, 0, 2, 3)  4.61 us

profile of v3, /device:TPU:0, one launch (start us, length us, event | category | flops | bytes accessed | tf_op | source)
XLA Modules:
  0.0 121.2 jit_solution(7707233557097623333)
XLA Ops:
  0.6 2.4 %pad_bitcast_fusion.1 = bf16[7,12,8,2048]{3,2,0,1:T(8,128)(2,1)S(1)} fusion(bf16[12,7,7,2048]{3,2,1,0:T(8,128)(2,1)} %param.7), kind=kLoop, calls=%fused_computation.3 | loop fusion | bytes 5160960 | tf_op jit(solution)/shard_map/transpose | solution.py:737
  3.0 0.0 copy-start
  3.0 1.7 %copy.11 = bf16[7,12,8,2048]{3,2,1,0:T(8,128)(2,1)} copy(bf16[7,12,8,2048]{3,2,0,1:T(8,128)(2,1)S(1)} %pad_bitcast_fusion.1) | data formatting | bytes 5505024 | tf_op jit(solution)/shard_map/transpose | solution.py:737
  4.8 1.0 copy-done
  5.8 0.7 pad_bitcast_fusion
  6.6 1.7 %copy.12 = bf16[7,12,8,2048]{3,2,1,0:T(8,128)(2,1)} copy(bf16[7,12,8,2048]{3,2,0,1:T(8,128)(2,1)S(1)} %pad_bitcast_fusion) | data formatting | bytes 5505024 | tf_op jit(solution)/shard_map/transpose | solution.py:737
  8.3 107.0 %block.1 = (bf16[672,2048]{1,0:T(8,128)(2,1)}, bf16[672,2048]{1,0:T(8,128)(2,1)}, f32[32,1088]{1,0:T(8,128)}, f32[2,3072]{1,0:T(2,128)}) custom-call(bf16[672,2048]{1,0:T(8,128)(2,1)} %bitcast.15, bf16[672,2048]{1,0:T(8,128)(2,1)} %bitcast.18, bf16[2048,512]{1,0:T(8,128)(2,1)} %wr_hbm.1, bf16[4608,512]{1,0:T(8,128)(2,1)} %ws_hbm.1, ...), custom_call_target="tpu_custom_call" | custom-call | flops 17999998976 | bytes 40000000 | tf_op jit(solution)/shard_map/block/pallas_call | solution.py:662
  115.3 0.0 copy-start.1
  115.3 0.0 copy-start.2
  115.3 4.6 %copy_bitcast_fusion = (bf16[12,7,7,2048]{3,2,1,0:T(8,128)(2,1)}, bf16[12,7,7,2048]{3,2,1,0:T(8,128)(2,1)}) fusion(bf16[7,12,8,2048]{3,2,1,0:T(8,128)(2,1)} %bitcast.16, bf16[7,12,8,2048]{3,2,1,0:T(8,128)(2,1)} %bitcast.17), kind=kLoop, calls=%fused_computation | loop fusion | bytes 10321920 | tf_op jit(solution)/shard_map/transpose | solution.py:741
  119.9 0.0 copy-done.1
  119.9 0.7 copy.21
  120.6 0.0 copy-done.2
  120.6 0.6 copy.22
Async XLA Ops:
  3.0 2.8 %copy-start = (bf16[12,7,7,2048]{3,2,1,0:T(8,128)(2,1)S(1)}, bf16[12,7,7,2048]{3,2,1,0:T(8,128)(2,1)}, u32[]{:S(2)}) copy-start(bf16[12,7,7,2048]{3,2,1,0:T(8,128)(2,1)} %param.8) | copy-start | bytes 7225348
  115.3 4.6 %copy-start.1 = (f32[32,1088]{1,0:T(8,128)S(1)}, f32[32,1088]{1,0:T(8,128)}, u32[]{:S(2)}) copy-start(f32[32,1088]{1,0:T(8,128)} %get-tuple-element.10) | copy-start | bytes 417796
  115.3 5.3 %copy-start.2 = (f32[2,3072]{1,0:T(2,128)S(1)}, f32[2,3072]{1,0:T(2,128)}, u32[]{:S(2)}) copy-start(f32[2,3072]{1,0:T(2,128)} %get-tuple-element.21) | copy-start | bytes 73732

commit v4 on v3

--- a/solution.py
+++ b/solution.py
@@ -78,10 +78,10 @@
 def block(
     x_hbm, cot_hbm, wr_hbm, ws_hbm, we_hbm, gain_ref, shift_ref,
     out_hbm, ing_hbm, wg_ref, norm_out,
-    x, cot, wa, ws, pre1, taps, pre2, h2, pre3, up, g3, g2, back, turned, stage, rows,
+    x, raw, wa, ws, pre1, taps, pre2, h2, pre3, up, g3, g2, back, turned, stage, rows,
     s1, s2, s3, s4, s5, s6, norm, own, other, ab1, ab2, ab3, ab4, c1, c2, c3, c4, last, ny, nx,
     load_sem, send_sem, recv_sem, out_sem, core_send, core_recv,
-    ab_send, ab_recv, cz_send, cz_recv, cd_send, cd_recv, last_send, last_recv, norm_send, norm_recv, ready,
+    ab_send, ab_recv, c_send, c_recv, last_send, last_recv, norm_send, norm_recv, ready,
 ):
     b, rep = lax.axis_index("bngroup"), lax.axis_index("rep")
     z, c = b // 2, b % 2
@@ -99,7 +99,15 @@
         copy.start()
         return copy
 
-    load_x = load(0, x_hbm, x)
+    def load_images(first, apart, images):
+        return [load(first + apart * r, images.at[:, r], raw.at[r]) for r in range(SIDE)]
+
+    def raw_rows(r, at):
+        value = raw[r, :, :, at].astype(F32)
+        value = jnp.concatenate([value, jnp.zeros((IMGS, 1, value.shape[2]), F32)], axis=1)
+        return value.reshape(BAND, value.shape[2])
+
+    load_x = load_images(6, 1, x_hbm)
     load_wr = load(1, wr_hbm, wa)
 
     barrier = pltpu.get_barrier_semaphore()
@@ -115,24 +123,19 @@
     g2[0:BAND, :] = zeros
     g2[ROWS + BAND :, :] = zeros
 
+    partner = {"bngroup": b + 1 - 2 * c}
+
+    def remote(src, dst, device, sems):
+        return pltpu.make_async_remote_copy(
+            src_ref=src, dst_ref=dst, send_sem=sems[0], recv_sem=sems[1],
+            device_id=device, device_id_type=MESH,
+        )
+
     def share(e, slots):
-        copies = []
+        sems = (send_sem.at[e], recv_sem.at[e])
         for k in range(1, GROUP):
-            copy = pltpu.make_async_remote_copy(
-                src_ref=slots.at[b],
-                dst_ref=slots.at[b],
-                send_sem=send_sem.at[e, k - 1],
-                recv_sem=recv_sem.at[e, k - 1],
-                device_id={"bngroup": (b + k) % GROUP},
-                device_id_type=MESH,
-            )
-            copy.start()
-            copies.append(copy)
-        return copies
-
-    def arrive(copies):
-        for copy in copies:
-            copy.wait()
+            remote(slots.at[b], slots.at[b], {"bngroup": (b + k) % GROUP}, sems).start()
+        return remote(slots.at[0 : GROUP - 1], slots.at[0 : GROUP - 1], partner, sems)
 
     CEN, AMP, SHI, INV, SS, GS = range(6)
     OFF = {1: 0, 2: MID, 3: 2 * MID}
@@ -188,11 +191,16 @@
         put(SS, which, shift_sum / COUNT)
         put(GS, which, inverse * gain_sum / COUNT)
 
-    load_x.wait()
+    for r in range(SIDE):
+        load_x[r].wait()
+
+        @pl.loop(0, WIDE // CH)
+        def _(j, r=r):
+            x[r * BAND : (r + 1) * BAND, lanes_at(j)] = raw_rows(r, lanes_at(j)).astype(BF16)
+
     load_wr.wait()
     load_ws = load(2, ws_hbm, ws)
-    load_cot = load(4, cot_hbm, cot)
-
+    load_images(4, 0, cot_hbm)
     @pl.loop(0, MID // CH)
     def _(j):
         pre1[:, lanes_at(j)] = dot(x[...], wa[:, lanes_at(j)])
@@ -200,7 +208,7 @@
 
     load_we = load(3, we_hbm, wa)
     pl.semaphore_wait(barrier, GROUP - 1 + 6)
-    arrive(share(0, s1))
+    share(0, s1).wait()
     group_stats(s1, 1)
 
     @pl.loop(0, MID // CH)
@@ -227,7 +235,14 @@
         pre2[:, lanes_at(j)] = real_rows(acc)
         stats(pre2, j, s2, MID)
 
-    arrive(share(1, s2))
+    sums = share(1, s2)
+
+    @pl.loop(0, 9)
+    def _(tap):
+        at = pl.ds(pl.multiple_of(tap * MID, MID), MID)
+        ws[at, :] = ws[at, :].T
+
+    sums.wait()
     group_stats(s2, 2)
 
     @pl.loop(0, MID // CH)
@@ -246,9 +261,9 @@
         pre3[:, lanes_at(j)] = dot(h2[...], wa[lanes_at(j), :], ((1,), (1,)))
         stats(pre3, j, s3, WIDE)
 
-    arrive(share(2, s3))
+    share(2, s3).wait()
     group_stats(s3, 3)
-    load_cot.wait()
+    pltpu.make_async_copy(raw, raw, load_sem.at[4]).wait()
 
     @pl.loop(0, WIDE // CH)
     def _(j):
@@ -260,8 +275,8 @@
             centred = pre3[band, at] - cen
             summed = centred * amp + shi + x[band, at].astype(F32)
             sigma = sigmoid(summed)
-            upstream = cot[band, at].astype(F32) * (sigma * (1.0 + summed * (1.0 - sigma)))
-            cot[band, at] = (summed * sigma).astype(BF16)
+            upstream = raw_rows(r, at) * (sigma * (1.0 + summed * (1.0 - sigma)))
+            g3[band, at] = (summed * sigma).astype(BF16)
             up[band, at] = upstream
             pre3[band, at] = centred
             return (acc[0] + fold_rows(upstream), acc[1] + fold_rows(upstream * centred))
@@ -283,28 +298,17 @@
             return pre3.at[256:512, at]
         return other.at[:, at]
 
+    names = list(PIECES)
+
     def to_partner(piece, i):
-        lane, size, chunk, _ = PIECES[piece]
-        start = LANDING[piece]
-        at = pl.ds(pl.multiple_of(start + i * MID, MID), MID)
-        return pltpu.make_async_remote_copy(
-            src_ref=stage.at[(chunk + i) % SLOTS],
-            dst_ref=landing(piece, at),
-            send_sem=core_send.at[chunk + i],
-            recv_sem=core_recv.at[chunk + i],
-            device_id={"bngroup": b + 1 - 2 * c},
-            device_id_type=MESH,
-        )
+        chunk = PIECES[piece][2]
+        at = pl.ds(pl.multiple_of(LANDING[piece] + i * MID, MID), MID)
+        slot = (chunk + i) % SLOTS
+        sems = (core_send.at[slot], core_recv.at[names.index(piece)])
+        return remote(stage.at[slot], landing(piece, at), partner, sems)
 
     def slot_free(n):
-        pltpu.make_async_remote_copy(
-            src_ref=stage.at[n % SLOTS],
-            dst_ref=other.at[:, 0:MID],
-            send_sem=core_send.at[n],
-            recv_sem=core_recv.at[n],
-            device_id={"bngroup": b + 1 - 2 * c},
-            device_id_type=MESH,
-        ).wait_send()
+        remote(stage.at[n % SLOTS], other.at[:, 0:MID], partner, (core_send.at[n % SLOTS], core_recv.at[0])).wait_send()
 
     def weigh(piece, right):
         lane, size, chunk, count = PIECES[piece]
@@ -324,17 +328,10 @@
     flying = {}
 
     def send(src, dst, device, sems):
-        copy = pltpu.make_async_remote_copy(
-            src_ref=src, dst_ref=dst, send_sem=sems[0], recv_sem=sems[1],
-            device_id=device, device_id_type=MESH,
-        )
-        copy.start()
-        return copy
+        remote(src, dst, device, sems).start()
 
     def plus(k, base):
         return (base + k) % 4
-
-    names = list(PIECES)
 
     def step(piece, n):
         lane, size, chunk, count = PIECES[piece]
@@ -342,10 +339,8 @@
         p = names.index(piece)
         half = width // 2
         if n == 0:
-            for i in range(count):
-                to_partner(piece, i).wait_recv()
-            start = LANDING[piece]
-            landed = landing(piece, pl.ds(start, size))
+            landed = landing(piece, pl.ds(LANDING[piece], size))
+            remote(landed, landed, partner, (core_send.at[0], core_recv.at[p])).wait_recv()
 
             @pl.loop(0, 16)
             def _(k):
@@ -354,7 +349,8 @@
         else:
             for copy in flying.pop((piece, n - 1)):
                 copy.wait()
-        copies = []
+        if n < 4:
+            ab_sems, c_sems = (ab_send.at[p, n], ab_recv.at[p, n]), (c_send.at[p, n], c_recv.at[p, n])
         for color in range(2):
             span = pl.ds(lane + color * width, width)
             local = pl.ds(ab_at, width)
@@ -362,7 +358,6 @@
             outer, inner = (xx, yy) if color == 0 else (yy, xx)
             parts = [pl.ds(lane + color * width + k * half, half) for k in range(2)]
             local_part = pl.ds(ab_at // 2, half)
-            sems = [(ab_send.at[p, color, n, side], ab_recv.at[p, color, n, side]) for side in range(2)] if n < 4 else None
 
             def outer_block(index, part=slice(None), color=color, span=span):
                 return own.at[index, part, :, span] if color == 0 else own.at[part, index, :, span]
@@ -372,28 +367,28 @@
 
             if n == 0:
                 far = plus(2, outer)
-                copies.append(send(outer_block(far, slice(0, 2)), ab1.at[color, 0, :, :, local], along(axes[0], 1), sems[0]))
-                copies.append(send(outer_block(far, slice(2, 4)), ab1.at[color, 1, :, :, local], along(axes[0], 3), sems[1]))
+                send(outer_block(far, slice(0, 2)), ab1.at[color, 0, :, :, local], along(axes[0], 1), ab_sems)
+                send(outer_block(far, slice(2, 4)), ab1.at[color, 1, :, :, local], along(axes[0], 3), ab_sems)
             elif n == 1:
                 low = outer_block(plus(1, outer), slice(0, 2))
                 low[...] += ab1[color, 0, :, :, local]
                 high = outer_block(plus(3, outer), slice(2, 4))
                 high[...] += ab1[color, 1, :, :, local]
-                copies.append(send(outer_block(plus(1, outer)), ab2.at[color, 0, :, :, local], along(axes[0], 1), sems[0]))
-                copies.append(send(outer_block(plus(3, outer)), ab2.at[color, 1, :, :, local], along(axes[0], 3), sems[1]))
+                send(outer_block(plus(1, outer)), ab2.at[color, 0, :, :, local], along(axes[0], 1), ab_sems)
+                send(outer_block(plus(3, outer)), ab2.at[color, 1, :, :, local], along(axes[0], 3), ab_sems)
             elif n == 2:
                 mine = outer_block(outer)
                 mine[...] += ab2[color, 0, :, :, local] + ab2[color, 1, :, :, local]
                 far = plus(2, inner)
-                copies.append(send(inner_block(far, parts[0]), ab3.at[color, 0, :, local_part], along(axes[1], 1), sems[0]))
-                copies.append(send(inner_block(far, parts[1]), ab3.at[color, 1, :, local_part], along(axes[1], 3), sems[1]))
+                send(inner_block(far, parts[0]), ab3.at[color, 0, :, local_part], along(axes[1], 1), ab_sems)
+                send(inner_block(far, parts[1]), ab3.at[color, 1, :, local_part], along(axes[1], 3), ab_sems)
             elif n == 3:
                 low = inner_block(plus(1, inner), parts[0])
                 low[...] += ab3[color, 0, :, local_part]
                 high = inner_block(plus(3, inner), parts[1])
                 high[...] += ab3[color, 1, :, local_part]
-                copies.append(send(inner_block(plus(1, inner), span), ab4.at[color, 0, :, local], along(axes[1], 1), sems[0]))
-                copies.append(send(inner_block(plus(3, inner), span), ab4.at[color, 1, :, local], along(axes[1], 3), sems[1]))
+                send(inner_block(plus(1, inner), span), ab4.at[color, 0, :, local], along(axes[1], 1), ab_sems)
+                send(inner_block(plus(3, inner), span), ab4.at[color, 1, :, local], along(axes[1], 3), ab_sems)
             else:
                 mine = inner_block(inner, span)
                 mine[...] += ab4[color, 0, :, local] + ab4[color, 1, :, local]
@@ -406,60 +401,45 @@
 
         first_axis = "x" if p % 2 == 0 else "y"
         second_axis = "y" if p % 2 == 0 else "x"
-        if n < 2:
-            sems = [(cz_send.at[p, n, side], cz_recv.at[p, n, side]) for side in range(2)]
-        elif n < 4:
-            sems = [(cd_send.at[p, n - 2, k], cd_recv.at[p, n - 2, k]) for k in range(3)]
         if n == 0:
             far = tile(plus(2, z))
-            copies.append(send(own.at[0:2, :, :, far], c1.at[0, :, :, :, local], along("z", 1), sems[0]))
-            copies.append(send(own.at[2:4, :, :, far], c1.at[1, :, :, :, local], along("z", 3), sems[1]))
+            send(own.at[0:2, :, :, far], c1.at[0, :, :, :, local], along("z", 1), c_sems)
+            send(own.at[2:4, :, :, far], c1.at[1, :, :, :, local], along("z", 3), c_sems)
         elif n == 1:
             up_one, down_one = tile(plus(1, z)), tile(plus(3, z))
             own[0:2, :, :, up_one] += c1[0, :, :, :, local]
             own[2:4, :, :, down_one] += c1[1, :, :, :, local]
-            copies.append(send(own.at[:, :, :, up_one], c2.at[0, :, :, :, local], along("z", 1), sems[0]))
-            copies.append(send(own.at[:, :, :, down_one], c2.at[1, :, :, :, local], along("z", 3), sems[1]))
+            send(own.at[:, :, :, up_one], c2.at[0, :, :, :, local], along("z", 1), c_sems)
+            send(own.at[:, :, :, down_one], c2.at[1, :, :, :, local], along("z", 3), c_sems)
         elif n == 2:
             own[:, :, :, tile(z)] += c2[0, :, :, :, local] + c2[1, :, :, :, local]
             for k in range(1, 4):
                 block_of = own.at[plus(k, xx), :, :, tile(z)] if p % 2 == 0 else own.at[:, plus(k, yy), :, tile(z)]
-                copies.append(send(block_of, c3.at[k - 1, :, :, local], along(first_axis, k), sems[k - 1]))
+                send(block_of, c3.at[k - 1, :, :, local], along(first_axis, k), c_sems)
         elif n == 3:
             mine = own.at[xx, :, :, tile(z)] if p % 2 == 0 else own.at[:, yy, :, tile(z)]
             mine[...] += c3[0, :, :, local] + c3[1, :, :, local] + c3[2, :, :, local]
             for k in range(1, 4):
                 block_of = own.at[xx, plus(k, yy), :, tile(z)] if p % 2 == 0 else own.at[plus(k, xx), yy, :, tile(z)]
-                copies.append(send(block_of, c4.at[k - 1, :, local], along(second_axis, k), sems[k - 1]))
+                send(block_of, c4.at[k - 1, :, local], along(second_axis, k), c_sems)
         else:
             mine = own[xx, yy, :, tile(z)] + c4[0, :, local] + c4[1, :, local] + c4[2, :, local]
             own[xx, yy, :, base : base + 512] = jnp.zeros((16, 512), F32)
             own[xx, yy, :, tile(z)] = mine
         if n < 4:
-            flying[piece, n] = copies
+            ab_local = pl.ds(ab_at // 2, half) if n == 2 else pl.ds(ab_at, width)
+            ab, third = (ab1, ab2, ab3, ab4)[n], (c1, c2, c3, c4)[n]
+            ab_whole = ab.at[:, :, :, :, ab_local] if n < 2 else ab.at[:, :, :, ab_local]
+            c_whole = third.at[:, :, :, :, local] if n < 2 else third.at[:, :, :, local] if n == 2 else third.at[:, :, local]
+            flying[piece, n] = [remote(ab_whole, ab_whole, partner, ab_sems), remote(c_whole, c_whole, partner, c_sems)]
 
     def owned(device):
         return pl.ds(pl.multiple_of((device // 2) * ZBLOCK + (device % 2) * 1024, 128), OWN)
 
+    last_sems = (last_send.at[0], last_recv.at[0])
+
     def to_owner(t):
-        return pltpu.make_async_remote_copy(
-            src_ref=own.at[xx, yy, :, owned(t)],
-            dst_ref=last.at[b],
-            send_sem=last_send.at[t],
-            recv_sem=last_recv.at[b],
-            device_id={"bngroup": t},
-            device_id_type=MESH,
-        )
-
-    def from_member(t):
-        return pltpu.make_async_remote_copy(
-            src_ref=own.at[xx, yy, :, owned(b)],
-            dst_ref=last.at[t],
-            send_sem=last_send.at[t],
-            recv_sem=last_recv.at[t],
-            device_id={"bngroup": t},
-            device_id_type=MESH,
-        )
+        return remote(own.at[xx, yy, :, owned(t)], last.at[b], {"bngroup": t}, last_sems)
 
     def to_owners(targets):
         for t in targets:
@@ -469,20 +449,21 @@
                 to_owner(t).start()
 
     def gather(n, axis, slots, mine):
-        return [
-            send(slots.at[mine], slots.at[mine], along(axis, k), (norm_send.at[n, k - 1], norm_recv.at[n, k - 1]))
-            for k in range(1, 4)
-        ]
+        sems = (norm_send.at[n], norm_recv.at[n])
+        for k in range(1, 4):
+            send(slots.at[mine], slots.at[mine], along(axis, k), sems)
+        return remote(slots.at[0:3], slots.at[0:3], partner, sems)
 
     def sum_of(slots):
         return slots[0] + slots[1] + slots[2] + slots[3]
 
     sums = share(3, s4)
-    write_out = pltpu.make_async_copy(cot, out_hbm, out_sem.at[0])
+    write_out = pltpu.make_async_copy(g3, out_hbm, out_sem.at[0])
     write_out.start()
     turn(h2[...])
-    arrive(sums)
+    sums.wait()
     group_sums(s4, 3)
+    write_out.wait()
 
     @pl.loop(0, WIDE // CH)
     def _(j):
@@ -530,7 +511,7 @@
     load_wr = load(5, wr_hbm, wa)
 
     step("expand", 0)
-    arrive(sums)
+    sums.wait()
     group_sums(s5, 2)
 
     @pl.loop(0, MID // CH)
@@ -553,32 +534,36 @@
     def back_one(j):
         acc = None
         for row in range(3):
-            for col in range(3):
-                left = g2[(2 - row) * BAND : (2 - row) * BAND + ROWS, col * MID : (col + 1) * MID]
-                at = pl.ds((3 * row + col) * MID + j * CH, CH)
-                part = dot(left, ws[at, :], ((1,), (1,)))
-                acc = part if acc is None else acc + part
+            left = g2[(2 - row) * BAND : (2 - row) * BAND + ROWS, :]
+            part = dot(left, ws[3 * MID * row : 3 * MID * (row + 1), j * CH : (j + 1) * CH])
+            acc = part if acc is None else acc + part
         back[:, j * CH : (j + 1) * CH] = acc
         slope_sums(pre1, 1, j, s6)
 
+    def input_gradient(quarter):
+        @pl.loop(2 * quarter, 2 * quarter + 2)
+        def _(j):
+            at = lanes_at(j)
+            g3[:, at] = (up[:, at] + dot(h2[...], wa[at, :], ((1,), (1,)))).astype(BF16)
+
     turn(g2[BAND : ROWS + BAND, MID : 2 * MID])
     weigh("low", tap_row(0))
+    step("expand", 1)
     weigh("mid", tap_row(1))
     step("low", 0)
-    step("expand", 1)
     weigh("high", tap_row(2))
     step("mid", 0)
     back_one(0)
     step("high", 0)
+    step("expand", 2)
     step("low", 1)
-    step("expand", 2)
     back_one(1)
     sums = share(5, s6)
     step("mid", 1)
+    step("high", 1)
     step("expand", 3)
-    step("high", 1)
     step("low", 2)
-    arrive(sums)
+    sums.wait()
     group_sums(s6, 1)
     ny[yy] = norm[...]
     norm_copies = gather(0, "y", ny, yy)
@@ -595,55 +580,43 @@
     step("upper", 0)
     step("mid", 2)
     step("first", 0)
+    load_wr.wait()
+    input_gradient(0)
     step("high", 2)
+    step("expand", 4)
+    step("upper", 1)
+    input_gradient(1)
     step("low", 3)
-    step("expand", 4)
-
-    load_wr.wait()
-
-    @pl.loop(0, WIDE // CH)
-    def _(j):
-        at = lanes_at(j)
-        g3[:, at] = (up[:, at] + dot(h2[...], wa[at, :], ((1,), (1,)))).astype(BF16)
-
+    step("first", 1)
+    input_gradient(2)
+    step("mid", 3)
+    step("upper", 2)
+    step("low", 4)
+    step("high", 3)
+    input_gradient(3)
     write_in = pltpu.make_async_copy(g3, ing_hbm, out_sem.at[1])
     write_in.start()
-
-    step("upper", 1)
-    step("mid", 3)
-    step("first", 1)
-    step("high", 3)
-    step("low", 4)
-    for copy in norm_copies:
-        copy.wait()
+    step("first", 2)
+    norm_copies.wait()
     nx[xx] = sum_of(ny)
     norm_copies = gather(1, "x", nx, xx)
-    step("upper", 2)
     step("mid", 4)
-    step("first", 2)
+    step("upper", 3)
     step("high", 4)
-    to_owners(range(2, 8))
-    step("upper", 3)
+    to_owners(range(2, GROUP))
     step("first", 3)
     step("upper", 4)
     to_owners(range(1, 2))
     step("first", 4)
-    to_owners(range(0, 1))
+    to_owners(range(1))
     last[b] = own[xx, yy, :, owned(b)]
 
-    for copy in norm_copies:
-        copy.wait()
+    norm_copies.wait()
     norm_out[...] = sum_of(nx) * (1.0 / IMAGES)
-    write_out.wait()
     write_in.wait()
     for n in range(13, 17):
         slot_free(n)
-    for t in range(GROUP):
-
-        @pl.when(b != t)
-        def _(t=t):
-            to_owner(t).wait_send()
-            from_member(t).wait_recv()
+    remote(last.at[0 : GROUP - 1], last.at[0 : GROUP - 1], partner, last_sems).wait()
 
     parts = []
     for core in range(2):
@@ -671,7 +644,7 @@
         out_specs=(any_, any_, vmem, vmem),
         scratch_shapes=[
             v((ROWS, WIDE), BF16),
-            v((ROWS, WIDE), BF16),
+            v((SIDE, IMGS, SIDE, WIDE), BF16),
             v((WIDE, MID), BF16),
             v((9 * MID, MID), BF16),
             v((ROWS, MID), F32),
@@ -706,22 +679,20 @@
             v((GROUP, 16, OWN), F32),
             v((4, 2, 3072), F32),
             v((4, 2, 3072), F32),
+            dma((6 + SIDE,)),
             dma((6,)),
-            dma((6, GROUP - 1)),
-            dma((6, GROUP - 1)),
+            dma((6,)),
             dma((2,)),
-            dma((17,)),
-            dma((17,)),
-            dma((pieces, 2, 4, 2)),
-            dma((pieces, 2, 4, 2)),
-            dma((pieces, 2, 2)),
-            dma((pieces, 2, 2)),
-            dma((pieces, 2, 3)),
-            dma((pieces, 2, 3)),
-            dma((GROUP,)),
-            dma((GROUP,)),
-            dma((2, 3)),
-            dma((2, 3)),
+            dma((SLOTS,)),
+            dma((pieces,)),
+            dma((pieces, 4)),
+            dma((pieces, 4)),
+            dma((pieces, 4)),
+            dma((pieces, 4)),
+            dma((1,)),
+            dma((1,)),
+            dma((2,)),
+            dma((2,)),
             pltpu.SemaphoreType.REGULAR,
         ],
         compiler_params=pltpu.CompilerParams(
@@ -732,18 +703,13 @@
     )(x, cot, wr, ws, we, gain, shift)
 
 
-def to_rows(images):
-    padded = jnp.pad(images, ((0, 0), (0, 0), (0, 1), (0, 0)))
-    return padded.transpose(1, 0, 2, 3).reshape(ROWS, WIDE)
-
-
 def from_rows(rows):
     return rows.reshape(SIDE, IMGS, COLS, WIDE)[:, :, :SIDE].transpose(1, 0, 2, 3)
 
 
 def per_device(images, cotangent, w_reduce, w_spatial, w_expand, norm_gain, norm_shift):
     output, in_grad, grads, norm_grads = run_block(
-        to_rows(images), to_rows(cotangent), w_reduce, w_spatial, w_expand,
+        images, cotangent, w_reduce, w_spatial, w_expand,
         norm_gain.reshape(1, -1), norm_shift.reshape(1, -1),
     )
     return (from_rows(output), from_rows(in_grad), grads.T, norm_grads)

time: 121 us -> 109 us (0.901)
  local copies, waits for them, and re-layouts: 13.5 us -> 5.89 us
  Pallas kernels: 107 us -> 102 us
    transpose x4 -> x0, local copies, waits for them, and re-layouts: 6.59 us -> none  [to_rows(): return padded.transpose(1, 0, 2, 3).reshape(ROWS, WIDE)]
    pallas_call x1, Pallas kernels: 107 us -> 102 us  [run_block(): pl.pallas_call(block, out_shape=(jax.ShapeDtypeStruct((ROWS, WIDE), BF16)...]
where the time goes in v4:
time: 109 us; the launch traced here: 108 us
  Pallas kernels  102 us (94%)
  local copies, waits for them, and re-layouts  5.89 us (5%)
    pallas_call x1, Pallas kernels, run_block(): pl.pallas_call(block, out_shape=(jax.ShapeDtypeStruct((ROWS, WIDE), BF16)...  102 us
    transpose x1, local copies, waits for them, and re-layouts, from_rows(): rows.reshape(SIDE, IMGS, COLS, WIDE)[:, :, :SIDE].transpose(1, 0, 2, 3)  4.61 us

profile of v4, /device:TPU:0, one launch (start us, length us, event | category | flops | bytes accessed | tf_op | source)
XLA Modules:
  0.0 108.5 jit_solution(8138733699494249546)
XLA Ops:
  0.6 101.9 %block.1 = (bf16[672,2048]{1,0:T(8,128)(2,1)}, bf16[672,2048]{1,0:T(8,128)(2,1)}, f32[32,1088]{1,0:T(8,128)}, f32[2,3072]{1,0:T(2,128)}) custom-call(bf16[12,7,7,2048]{3,2,1,0:T(8,128)(2,1)} %x_hbm.1, bf16[12,7,7,2048]{3,2,1,0:T(8,128)(2,1)} %cot_hbm.1, bf16[2048,512]{1,0:T(8,128)(2,1)} %wr_hbm.1, bf16[4608,512]{1,0:T(8,128)(2,1)} %ws_hbm.1, ...), custom_call_target="tpu_custom_call" | custom-call | flops 17999998976 | bytes 40000000 | tf_op jit(solution)/shard_map/block/pallas_call | solution.py:635
  102.6 0.0 copy-start
  102.6 0.0 copy-start.1
  102.6 4.6 %copy_bitcast_fusion = (bf16[12,7,7,2048]{3,2,1,0:T(8,128)(2,1)}, bf16[12,7,7,2048]{3,2,1,0:T(8,128)(2,1)}) fusion(bf16[7,12,8,2048]{3,2,1,0:T(8,128)(2,1)} %bitcast.9, bf16[7,12,8,2048]{3,2,1,0:T(8,128)(2,1)} %bitcast.10), kind=kLoop, calls=%fused_computation | loop fusion | bytes 10321920 | tf_op jit(solution)/shard_map/transpose | solution.py:707
  107.2 0.0 copy-done
  107.2 0.7 copy.19
  107.9 0.0 copy-done.1
  107.9 0.6 copy.20
Async XLA Ops:
  102.6 4.6 %copy-start = (f32[32,1088]{1,0:T(8,128)S(1)}, f32[32,1088]{1,0:T(8,128)}, u32[]{:S(2)}) copy-start(f32[32,1088]{1,0:T(8,128)} %get-tuple-element.10) | copy-start | bytes 417796
  102.6 5.3 %copy-start.1 = (f32[2,3072]{1,0:T(2,128)S(1)}, f32[2,3072]{1,0:T(2,128)}, u32[]{:S(2)}) copy-start(f32[2,3072]{1,0:T(2,128)} %get-tuple-element.21) | copy-start | bytes 73732

commit v5 on v4

--- a/solution.py
+++ b/solution.py
@@ -26,20 +26,25 @@
 SLOTS = 4
 
 PIECES = {
-    "expand": (6656, 2048, 0, 4),
+    "expand": (6656, 1024, 0, 2),
+    "extra": (7680, 1024, 2, 2),
     "low": (2048, 1536, 4, 3),
     "mid": (3584, 1536, 7, 3),
     "high": (5120, 1536, 10, 3),
     "upper": (1024, 1024, 13, 2),
     "first": (0, 1024, 15, 2),
 }
-LANDING = {"expand": 0, "low": 0, "mid": 1536, "high": 3072, "upper": 1024, "first": 0}
+LANDING = {"expand": 0, "extra": 1024, "low": 0, "mid": 1536, "high": 3072, "upper": 1024, "first": 0}
+THIRD = {"expand": 1, "low": 1, "mid": 1, "high": 1, "upper": 1, "first": 1}
+DIRECT = ("upper", "first",)
 SHARE = {}
-_ab, _c = 0, 0
+_ab, _c, _d = 0, 0, 0
 for _name, (_lane, _size, _, _) in PIECES.items():
-    _n = (_size - 512) // 2
-    SHARE[_name] = (_n, _ab, _c)
-    _ab, _c = _ab + _n, _c + 128
+    _n = (_size - 512 * THIRD.get(_name, 0)) // 2
+    SHARE[_name] = (_n, _ab, _c, _d)
+    _ab, _c, _d = _ab + _n, _c + 128 * THIRD.get(_name, 0), _d + (_n if _name in DIRECT else 0)
+EVEN = (0, 2, 4, 6)
+D_LANES = _d
 AB_LANES, C_LANES = _ab, _c
 
 
@@ -79,7 +84,7 @@
     x_hbm, cot_hbm, wr_hbm, ws_hbm, we_hbm, gain_ref, shift_ref,
     out_hbm, ing_hbm, wg_ref, norm_out,
     x, raw, wa, ws, pre1, taps, pre2, h2, pre3, up, g3, g2, back, turned, stage, rows,
-    s1, s2, s3, s4, s5, s6, norm, own, other, ab1, ab2, ab3, ab4, c1, c2, c3, c4, last, ny, nx,
+    s1, s2, s3, s4, s5, s6, norm, own, other, ab1, ab2, ab3, ab4, straight, c1, c2, c3, c4, last, ny, nx,
     load_sem, send_sem, recv_sem, out_sem, core_send, core_recv,
     ab_send, ab_recv, c_send, c_recv, last_send, last_recv, norm_send, norm_recv, ready,
 ):
@@ -147,21 +152,13 @@
     def get(row, which, j):
         return rows[row, :, pl.ds(pl.multiple_of(OFF[which] + j * CH, CH), CH)]
 
-    def stats(pre, j, slots, channels):
-        at = lanes_at(j)
-
-        def add(r, acc):
-            return acc + fold_rows(pre[band_at(r), at])
-
-        mean = total(lax.fori_loop(0, SIDE, add, jnp.zeros((8, CH), F32))) / REAL
-
-        def spread(r, acc):
-            off = real_rows(pre[band_at(r), at] - mean)
-            return acc + fold_rows(off * off)
-
-        second = total(lax.fori_loop(0, SIDE, spread, jnp.zeros((8, CH), F32)))
-        slots[b, :, at] = mean
-        slots[b, :, pl.ds(pl.multiple_of(channels + j * CH, CH), CH)] = second
+    def stats(value, j, slots, channels):
+        about = total(value[0:8]) / 7.0
+        off = real_rows(value - about)
+        first, second = total(fold_rows(off)) / REAL, total(fold_rows(off * off))
+        slots[b, :, lanes_at(j)] = about + first
+        at = pl.ds(pl.multiple_of(channels + j * CH, CH), CH)
+        slots[b, :, at] = jnp.maximum(second - REAL * (first * first), 0.0)
 
     def group_stats(slots, which):
         c = SIZE[which]
@@ -203,8 +200,9 @@
     load_images(4, 0, cot_hbm)
     @pl.loop(0, MID // CH)
     def _(j):
-        pre1[:, lanes_at(j)] = dot(x[...], wa[:, lanes_at(j)])
-        stats(pre1, j, s1, MID)
+        value = dot(x[...], wa[:, lanes_at(j)])
+        pre1[:, lanes_at(j)] = value
+        stats(value, j, s1, MID)
 
     load_we = load(3, we_hbm, wa)
     pl.semaphore_wait(barrier, GROUP - 1 + 6)
@@ -232,8 +230,9 @@
         acc = dot(taps[0:ROWS, :], ws[0 : 3 * MID, lanes_at(j)])
         acc = acc + dot(taps[BAND : ROWS + BAND, :], ws[3 * MID : 6 * MID, lanes_at(j)])
         acc = acc + dot(taps[2 * BAND :, :], ws[6 * MID :, lanes_at(j)])
-        pre2[:, lanes_at(j)] = real_rows(acc)
-        stats(pre2, j, s2, MID)
+        value = real_rows(acc)
+        pre2[:, lanes_at(j)] = value
+        stats(value, j, s2, MID)
 
     sums = share(1, s2)
 
@@ -258,8 +257,9 @@
 
     @pl.loop(0, WIDE // CH)
     def _(j):
-        pre3[:, lanes_at(j)] = dot(h2[...], wa[lanes_at(j), :], ((1,), (1,)))
-        stats(pre3, j, s3, WIDE)
+        value = dot(h2[...], wa[lanes_at(j), :], ((1,), (1,)))
+        pre3[:, lanes_at(j)] = value
+        stats(value, j, s3, WIDE)
 
     share(2, s3).wait()
     group_stats(s3, 3)
@@ -275,8 +275,9 @@
             centred = pre3[band, at] - cen
             summed = centred * amp + shi + x[band, at].astype(F32)
             sigma = sigmoid(summed)
-            upstream = raw_rows(r, at) * (sigma * (1.0 + summed * (1.0 - sigma)))
-            g3[band, at] = (summed * sigma).astype(BF16)
+            value = summed * sigma
+            upstream = raw_rows(r, at) * (sigma + value * (1.0 - sigma))
+            g3[band, at] = value.astype(BF16)
             up[band, at] = upstream
             pre3[band, at] = centred
             return (acc[0] + fold_rows(upstream), acc[1] + fold_rows(upstream * centred))
@@ -292,7 +293,7 @@
             turned[(half + c + 1) % 2] = halves[:, half].reshape(MID // 2, ROWS)
 
     def landing(piece, at):
-        if piece == "expand":
+        if piece in ("expand", "extra"):
             return pre3.at[0:256, at]
         if piece in ("upper", "first"):
             return pre3.at[256:512, at]
@@ -335,7 +336,8 @@
 
     def step(piece, n):
         lane, size, chunk, count = PIECES[piece]
-        width, ab_at, c_at = SHARE[piece]
+        width, ab_at, c_at, d_at = SHARE[piece]
+        direct = piece in DIRECT
         p = names.index(piece)
         half = width // 2
         if n == 0:
@@ -347,10 +349,9 @@
                 own[k // 4, k % 4, :, lane : lane + size] += landed[pl.ds(pl.multiple_of(k * 16, 16), 16), :]
 
         else:
-            for copy in flying.pop((piece, n - 1)):
-                copy.wait()
+            flying.pop((piece, n - 1)).wait()
         if n < 4:
-            ab_sems, c_sems = (ab_send.at[p, n], ab_recv.at[p, n]), (c_send.at[p, n], c_recv.at[p, n])
+            sems = (ab_send.at[p], ab_recv.at[p, n])
         for color in range(2):
             span = pl.ds(lane + color * width, width)
             local = pl.ds(ab_at, width)
@@ -367,71 +368,97 @@
 
             if n == 0:
                 far = plus(2, outer)
-                send(outer_block(far, slice(0, 2)), ab1.at[color, 0, :, :, local], along(axes[0], 1), ab_sems)
-                send(outer_block(far, slice(2, 4)), ab1.at[color, 1, :, :, local], along(axes[0], 3), ab_sems)
+                send(outer_block(far, slice(0, 2)), ab1.at[color, 0, :, :, local], along(axes[0], 1), sems)
+                send(outer_block(far, slice(2, 4)), ab1.at[color, 1, :, :, local], along(axes[0], 3), sems)
             elif n == 1:
                 low = outer_block(plus(1, outer), slice(0, 2))
                 low[...] += ab1[color, 0, :, :, local]
                 high = outer_block(plus(3, outer), slice(2, 4))
                 high[...] += ab1[color, 1, :, :, local]
-                send(outer_block(plus(1, outer)), ab2.at[color, 0, :, :, local], along(axes[0], 1), ab_sems)
-                send(outer_block(plus(3, outer)), ab2.at[color, 1, :, :, local], along(axes[0], 3), ab_sems)
+                send(outer_block(plus(1, outer)), ab2.at[color, 0, :, :, local], along(axes[0], 1), sems)
+                send(outer_block(plus(3, outer)), ab2.at[color, 1, :, :, local], along(axes[0], 3), sems)
             elif n == 2:
                 mine = outer_block(outer)
                 mine[...] += ab2[color, 0, :, :, local] + ab2[color, 1, :, :, local]
+                if direct:
+                    for k in range(1, 4):
+                        send(inner_block(plus(k, inner), span), straight.at[color, k - 1, :, pl.ds(d_at, width)], along(axes[1], k), sems)
+                    continue
                 far = plus(2, inner)
-                send(inner_block(far, parts[0]), ab3.at[color, 0, :, local_part], along(axes[1], 1), ab_sems)
-                send(inner_block(far, parts[1]), ab3.at[color, 1, :, local_part], along(axes[1], 3), ab_sems)
+                send(inner_block(far, parts[0]), ab3.at[color, 0, :, local_part], along(axes[1], 1), sems)
+                send(inner_block(far, parts[1]), ab3.at[color, 1, :, local_part], along(axes[1], 3), sems)
+            elif direct:
+                if n == 3:
+                    at = pl.ds(d_at, width)
+                    mine = inner_block(inner, span)
+                    mine[...] += straight[color, 0, :, at] + straight[color, 1, :, at] + straight[color, 2, :, at]
             elif n == 3:
                 low = inner_block(plus(1, inner), parts[0])
                 low[...] += ab3[color, 0, :, local_part]
                 high = inner_block(plus(3, inner), parts[1])
                 high[...] += ab3[color, 1, :, local_part]
-                send(inner_block(plus(1, inner), span), ab4.at[color, 0, :, local], along(axes[1], 1), ab_sems)
-                send(inner_block(plus(3, inner), span), ab4.at[color, 1, :, local], along(axes[1], 3), ab_sems)
+                send(inner_block(plus(1, inner), span), ab4.at[color, 0, :, local], along(axes[1], 1), sems)
+                send(inner_block(plus(3, inner), span), ab4.at[color, 1, :, local], along(axes[1], 3), sems)
             else:
                 mine = inner_block(inner, span)
                 mine[...] += ab4[color, 0, :, local] + ab4[color, 1, :, local]
-
+        if n < (3 if direct else 4):
+            if direct and n == 2:
+                ab = straight.at[:, :, :, pl.ds(d_at, width)]
+            elif n == 2:
+                ab = ab3.at[:, :, :, pl.ds(ab_at // 2, half)]
+            elif n == 3:
+                ab = ab4.at[:, :, :, pl.ds(ab_at, width)]
+            else:
+                ab = (ab1, ab2)[n].at[:, :, :, :, pl.ds(ab_at, width)]
+            flying[piece, n] = remote(ab, ab, partner, sems)
+
+    def third_step(piece, n):
+        lane = PIECES[piece][0]
+        width, _, c_at, _ = SHARE[piece]
+        p = names.index(piece)
         base = lane + 2 * width
-        local = pl.ds(c_at, 128)
+        tiles = 128 * THIRD[piece]
+        local = pl.ds(c_at, tiles)
+        if n > 0:
+            flying.pop((piece, n - 1, "third")).wait()
+        if n < 4:
+            sems = (c_send.at[p], c_recv.at[p, n])
 
         def tile(index):
-            return pl.ds(pl.multiple_of(base + 128 * index, 128), 128)
-
-        first_axis = "x" if p % 2 == 0 else "y"
-        second_axis = "y" if p % 2 == 0 else "x"
+            return pl.ds(pl.multiple_of(base + tiles * index, 128), tiles)
+
+        first_axis = "x" if p in EVEN else "y"
+        second_axis = "y" if p in EVEN else "x"
         if n == 0:
             far = tile(plus(2, z))
-            send(own.at[0:2, :, :, far], c1.at[0, :, :, :, local], along("z", 1), c_sems)
-            send(own.at[2:4, :, :, far], c1.at[1, :, :, :, local], along("z", 3), c_sems)
+            send(own.at[0:2, :, :, far], c1.at[0, :, :, :, local], along("z", 1), sems)
+            send(own.at[2:4, :, :, far], c1.at[1, :, :, :, local], along("z", 3), sems)
         elif n == 1:
             up_one, down_one = tile(plus(1, z)), tile(plus(3, z))
             own[0:2, :, :, up_one] += c1[0, :, :, :, local]
             own[2:4, :, :, down_one] += c1[1, :, :, :, local]
-            send(own.at[:, :, :, up_one], c2.at[0, :, :, :, local], along("z", 1), c_sems)
-            send(own.at[:, :, :, down_one], c2.at[1, :, :, :, local], along("z", 3), c_sems)
+            send(own.at[:, :, :, up_one], c2.at[0, :, :, :, local], along("z", 1), sems)
+            send(own.at[:, :, :, down_one], c2.at[1, :, :, :, local], along("z", 3), sems)
         elif n == 2:
             own[:, :, :, tile(z)] += c2[0, :, :, :, local] + c2[1, :, :, :, local]
             for k in range(1, 4):
-                block_of = own.at[plus(k, xx), :, :, tile(z)] if p % 2 == 0 else own.at[:, plus(k, yy), :, tile(z)]
-                send(block_of, c3.at[k - 1, :, :, local], along(first_axis, k), c_sems)
+                block_of = own.at[plus(k, xx), :, :, tile(z)] if p in EVEN else own.at[:, plus(k, yy), :, tile(z)]
+                send(block_of, c3.at[k - 1, :, :, local], along(first_axis, k), sems)
         elif n == 3:
-            mine = own.at[xx, :, :, tile(z)] if p % 2 == 0 else own.at[:, yy, :, tile(z)]
+            mine = own.at[xx, :, :, tile(z)] if p in EVEN else own.at[:, yy, :, tile(z)]
             mine[...] += c3[0, :, :, local] + c3[1, :, :, local] + c3[2, :, :, local]
             for k in range(1, 4):
-                block_of = own.at[xx, plus(k, yy), :, tile(z)] if p % 2 == 0 else own.at[plus(k, xx), yy, :, tile(z)]
-                send(block_of, c4.at[k - 1, :, local], along(second_axis, k), c_sems)
+                block_of = own.at[xx, plus(k, yy), :, tile(z)] if p in EVEN else own.at[plus(k, xx), yy, :, tile(z)]
+                send(block_of, c4.at[k - 1, :, local], along(second_axis, k), sems)
         else:
             mine = own[xx, yy, :, tile(z)] + c4[0, :, local] + c4[1, :, local] + c4[2, :, local]
-            own[xx, yy, :, base : base + 512] = jnp.zeros((16, 512), F32)
+            own[xx, yy, :, base : base + 4 * tiles] = jnp.zeros((16, 4 * tiles), F32)
             own[xx, yy, :, tile(z)] = mine
         if n < 4:
-            ab_local = pl.ds(ab_at // 2, half) if n == 2 else pl.ds(ab_at, width)
-            ab, third = (ab1, ab2, ab3, ab4)[n], (c1, c2, c3, c4)[n]
-            ab_whole = ab.at[:, :, :, :, ab_local] if n < 2 else ab.at[:, :, :, ab_local]
-            c_whole = third.at[:, :, :, :, local] if n < 2 else third.at[:, :, :, local] if n == 2 else third.at[:, :, local]
-            flying[piece, n] = [remote(ab_whole, ab_whole, partner, ab_sems), remote(c_whole, c_whole, partner, c_sems)]
+            whole = (c1, c2, c3, c4)[n]
+            whole = whole.at[:, :, :, :, local] if n < 2 else whole.at[:, :, :, local] if n == 2 else whole.at[:, :, local]
+            flying[piece, n, "third"] = remote(whole, whole, partner, sems)
 
     def owned(device):
         return pl.ds(pl.multiple_of((device // 2) * ZBLOCK + (device % 2) * 1024, 128), OWN)
@@ -499,21 +526,21 @@
         cen, amp, ss, gs = get(CEN, which, j), get(AMP, which, j), get(SS, which, j), get(GS, which, j)
         return real_rows(amp * (back[band, at] - ss - (pre[band, at] - cen) * gs))
 
-    pl.semaphore_signal(ready, inc=1, device_id={"bngroup": b + 1 - 2 * c}, device_id_type=MESH)
+    @pl.loop(0, MID // CH)
+    def _(j):
+        back[:, lanes_at(j)] = dot(g3[...], wa[:, lanes_at(j)])
+        slope_sums(pre2, 2, j, s5)
+
+    load_wr = load(5, wr_hbm, wa)
+
+    sums = share(4, s5)
+    pl.semaphore_signal(ready, inc=1, device_id=partner, device_id_type=MESH)
     pl.semaphore_wait(ready, 1)
     weigh("expand", lambda i, half: g3[:, pl.ds(pl.multiple_of(i * MID + half * CH, CH), CH)])
-    @pl.loop(0, MID // CH)
-    def _(j):
-        back[:, lanes_at(j)] = dot(g3[...], wa[:, lanes_at(j)])
-        slope_sums(pre2, 2, j, s5)
-
-    sums = share(4, s5)
-    load_wr = load(5, wr_hbm, wa)
-
+    weigh("extra", lambda i, half: g3[:, pl.ds(pl.multiple_of(1024 + i * MID + half * CH, CH), CH)])
     step("expand", 0)
     sums.wait()
     group_sums(s5, 2)
-
     @pl.loop(0, MID // CH)
     def _(j):
         @pl.loop(0, SIDE)
@@ -548,20 +575,28 @@
 
     turn(g2[BAND : ROWS + BAND, MID : 2 * MID])
     weigh("low", tap_row(0))
+    step("extra", 0)
+    weigh("mid", tap_row(1))
     step("expand", 1)
-    weigh("mid", tap_row(1))
     step("low", 0)
+    third_step("expand", 0)
+    third_step("low", 0)
     weigh("high", tap_row(2))
     step("mid", 0)
+    third_step("mid", 0)
+    step("extra", 1)
     back_one(0)
+    step("low", 1)
+    third_step("low", 1)
     step("high", 0)
-    step("expand", 2)
-    step("low", 1)
     back_one(1)
     sums = share(5, s6)
+    step("extra", 2)
     step("mid", 1)
-    step("high", 1)
-    step("expand", 3)
+    step("expand", 2)
+    third_step("mid", 1)
+    third_step("high", 0)
+    third_step("expand", 1)
     step("low", 2)
     sums.wait()
     group_sums(s6, 1)
@@ -574,41 +609,67 @@
         def _(r):
             h2[band_at(r), lanes_at(j)] = norm_back(pre1, 1, j, r).astype(BF16)
 
+    step("extra", 3)
+    step("high", 1)
+    third_step("low", 2)
     turn(h2[...])
     weigh("upper", lambda i, half: x[:, pl.ds(pl.multiple_of(1024 + i * MID + half * CH, CH), CH)])
+    third_step("mid", 2)
     weigh("first", lambda i, half: x[:, pl.ds(pl.multiple_of(i * MID + half * CH, CH), CH)])
     step("upper", 0)
+    third_step("upper", 0)
+    load_wr.wait()
+    input_gradient(0)
+    third_step("high", 1)
+    step("expand", 3)
     step("mid", 2)
     step("first", 0)
-    load_wr.wait()
-    input_gradient(0)
     step("high", 2)
+    third_step("first", 0)
+    third_step("upper", 1)
+    step("low", 3)
+    third_step("expand", 2)
+    third_step("mid", 3)
+    input_gradient(1)
+    step("mid", 3)
+    third_step("low", 3)
+    third_step("high", 2)
+    input_gradient(2)
     step("expand", 4)
+    step("first", 1)
+    step("low", 4)
+    step("extra", 4)
+    norm_copies.wait()
+    nx[xx] = sum_of(ny)
+    norm_copies = gather(1, "x", nx, xx)
     step("upper", 1)
-    input_gradient(1)
-    step("low", 3)
-    step("first", 1)
-    input_gradient(2)
-    step("mid", 3)
+    third_step("first", 1)
+    step("high", 3)
+    third_step("upper", 2)
+    third_step("mid", 4)
+    step("mid", 4)
+    third_step("high", 3)
+    third_step("low", 4)
+    to_owners(range(2, 4))
+    third_step("expand", 3)
+    third_step("first", 2)
     step("upper", 2)
-    step("low", 4)
-    step("high", 3)
+    third_step("high", 4)
+    third_step("expand", 4)
+    step("high", 4)
+    to_owners(range(4, GROUP))
+    third_step("upper", 3)
+    step("first", 2)
+    third_step("first", 3)
+    step("upper", 3)
+    third_step("upper", 4)
+    to_owners(range(1, 2))
+    step("first", 3)
+    third_step("first", 4)
+    to_owners(range(1))
     input_gradient(3)
     write_in = pltpu.make_async_copy(g3, ing_hbm, out_sem.at[1])
     write_in.start()
-    step("first", 2)
-    norm_copies.wait()
-    nx[xx] = sum_of(ny)
-    norm_copies = gather(1, "x", nx, xx)
-    step("mid", 4)
-    step("upper", 3)
-    step("high", 4)
-    to_owners(range(2, GROUP))
-    step("first", 3)
-    step("upper", 4)
-    to_owners(range(1, 2))
-    step("first", 4)
-    to_owners(range(1))
     last[b] = own[xx, yy, :, owned(b)]
 
     norm_copies.wait()
@@ -672,6 +733,7 @@
             v((2, 2, 4, 16, AB_LANES), F32),
             v((2, 2, 16, AB_LANES // 2), F32),
             v((2, 2, 16, AB_LANES), F32),
+            v((2, 3, 16, D_LANES), F32),
             v((2, 2, 4, 16, C_LANES), F32),
             v((2, 4, 4, 16, C_LANES), F32),
             v((3, 4, 16, C_LANES), F32),
@@ -685,9 +747,9 @@
             dma((2,)),
             dma((SLOTS,)),
             dma((pieces,)),
+            dma((pieces,)),
             dma((pieces, 4)),
-            dma((pieces, 4)),
-            dma((pieces, 4)),
+            dma((pieces,)),
             dma((pieces, 4)),
             dma((1,)),
             dma((1,)),

time: 109 us -> 103 us (0.945)
  Pallas kernels: 102 us -> 96.4 us
    pallas_call x1, Pallas kernels: 102 us -> 96.4 us  [run_block(): pl.pallas_call(block, out_shape=(jax.ShapeDtypeStruct((ROWS, WIDE), BF16)...]
where the time goes in v5:
time: 103 us
  Pallas kernels  96.4 us (94%)
  local copies, waits for them, and re-layouts  5.89 us (6%)
    pallas_call x1, Pallas kernels, run_block(): pl.pallas_call(block, out_shape=(jax.ShapeDtypeStruct((ROWS, WIDE), BF16)...  96.4 us
    transpose x1, local copies, waits for them, and re-layouts, from_rows(): rows.reshape(SIDE, IMGS, COLS, WIDE)[:, :, :SIDE].transpose(1, 0, 2, 3)  4.61 us

profile of v5, /device:TPU:0, one launch (start us, length us, event | category | flops | bytes accessed | tf_op | source)
XLA Modules:
  0.0 103.0 jit_solution(12780470395004111585)
XLA Ops:
  0.6 96.4 %block.1 = (bf16[672,2048]{1,0:T(8,128)(2,1)}, bf16[672,2048]{1,0:T(8,128)(2,1)}, f32[32,1088]{1,0:T(8,128)}, f32[2,3072]{1,0:T(2,128)}) custom-call(bf16[12,7,7,2048]{3,2,1,0:T(8,128)(2,1)} %x_hbm.1, bf16[12,7,7,2048]{3,2,1,0:T(8,128)(2,1)} %cot_hbm.1, bf16[2048,512]{1,0:T(8,128)(2,1)} %wr_hbm.1, bf16[4608,512]{1,0:T(8,128)(2,1)} %ws_hbm.1, ...), custom_call_target="tpu_custom_call" | custom-call | flops 17999998976 | bytes 40000000 | tf_op jit(solution)/shard_map/block/pallas_call | solution.py:696
  97.1 0.0 copy-start
  97.1 0.0 copy-start.1
  97.1 4.6 %copy_bitcast_fusion = (bf16[12,7,7,2048]{3,2,1,0:T(8,128)(2,1)}, bf16[12,7,7,2048]{3,2,1,0:T(8,128)(2,1)}) fusion(bf16[7,12,8,2048]{3,2,1,0:T(8,128)(2,1)} %bitcast.9, bf16[7,12,8,2048]{3,2,1,0:T(8,128)(2,1)} %bitcast.10), kind=kLoop, calls=%fused_computation | loop fusion | bytes 10321920 | tf_op jit(solution)/shard_map/transpose | solution.py:769
  101.7 0.0 copy-done
  101.7 0.7 copy.19
  102.4 0.0 copy-done.1
  102.4 0.6 copy.20
Async XLA Ops:
  97.1 4.6 %copy-start = (f32[32,1088]{1,0:T(8,128)S(1)}, f32[32,1088]{1,0:T(8,128)}, u32[]{:S(2)}) copy-start(f32[32,1088]{1,0:T(8,128)} %get-tuple-element.10) | copy-start | bytes 417796
  97.1 5.3 %copy-start.1 = (f32[2,3072]{1,0:T(2,128)S(1)}, f32[2,3072]{1,0:T(2,128)}, u32[]{:S(2)}) copy-start(f32[2,3072]{1,0:T(2,128)} %get-tuple-element.21) | copy-start | bytes 73732

commit v6 on v5

--- a/solution.py
+++ b/solution.py
@@ -11,6 +11,7 @@
 
 IMGS, SIDE, COLS = 12, 7, 8
 WIDE, MID = 2048, 512
+QUARTERS = 4
 BAND = IMGS * COLS
 ROWS = SIDE * BAND
 REAL = IMGS * SIDE * SIDE
@@ -144,10 +145,9 @@
 
     CEN, AMP, SHI, INV, SS, GS = range(6)
     OFF = {1: 0, 2: MID, 3: 2 * MID}
-    SIZE = {1: MID, 2: MID, 3: WIDE}
-
-    def put(row, which, value):
-        rows[row, :, OFF[which] : OFF[which] + SIZE[which]] = value
+
+    def put(row, off, value):
+        rows[row, :, off : off + value.shape[1]] = value
 
     def get(row, which, j):
         return rows[row, :, pl.ds(pl.multiple_of(OFF[which] + j * CH, CH), CH)]
@@ -160,8 +160,8 @@
         at = pl.ds(pl.multiple_of(channels + j * CH, CH), CH)
         slots[b, :, at] = jnp.maximum(second - REAL * (first * first), 0.0)
 
-    def group_stats(slots, which):
-        c = SIZE[which]
+    def group_stats(slots, which, start=0, c=MID):
+        off_at = OFF[which] + start
         mean = slots[0, :, 0:c]
         for i in range(1, GROUP):
             mean = mean + slots[i, :, 0:c]
@@ -171,22 +171,22 @@
             off = slots[i, :, 0:c] - mean
             second = second + (slots[i, :, c : 2 * c] + REAL * (off * off))
         inverse = lax.rsqrt(second / COUNT + EPS)
-        put(CEN, which, mean)
-        put(INV, which, inverse)
-        put(AMP, which, gain_ref[:, OFF[which] : OFF[which] + c] * inverse)
-        put(SHI, which, shift_ref[:, OFF[which] : OFF[which] + c])
-
-    def group_sums(slots, which):
-        c = SIZE[which]
+        put(CEN, off_at, mean)
+        put(INV, off_at, inverse)
+        put(AMP, off_at, gain_ref[:, off_at : off_at + c] * inverse)
+        put(SHI, off_at, shift_ref[:, off_at : off_at + c])
+
+    def group_sums(slots, which, start=0, c=MID):
+        off_at = OFF[which] + start
         sums = slots[0]
         for i in range(1, GROUP):
             sums = sums + slots[i]
         shift_sum, gain_sum = sums[:, 0:c], sums[:, c : 2 * c]
-        inverse = rows[INV, :, OFF[which] : OFF[which] + c]
-        norm[0:1, OFF[which] : OFF[which] + c] = gain_sum
-        norm[1:2, OFF[which] : OFF[which] + c] = shift_sum
-        put(SS, which, shift_sum / COUNT)
-        put(GS, which, inverse * gain_sum / COUNT)
+        inverse = rows[INV, :, off_at : off_at + c]
+        norm[0:1, off_at : off_at + c] = gain_sum
+        norm[1:2, off_at : off_at + c] = shift_sum
+        put(SS, off_at, shift_sum / COUNT)
+        put(GS, off_at, inverse * gain_sum / COUNT)
 
     for r in range(SIDE):
         load_x[r].wait()
@@ -255,37 +255,51 @@
 
     load_we.wait()
 
-    @pl.loop(0, WIDE // CH)
-    def _(j):
-        value = dot(h2[...], wa[lanes_at(j), :], ((1,), (1,)))
-        pre3[:, lanes_at(j)] = value
-        stats(value, j, s3, WIDE)
-
-    share(2, s3).wait()
-    group_stats(s3, 3)
+    exchanged = []
+    for q in range(QUARTERS):
+
+        @pl.loop(2 * q, 2 * q + 2)
+        def _(j, q=q):
+            value = dot(h2[...], wa[lanes_at(j), :], ((1,), (1,)))
+            pre3[:, lanes_at(j)] = value
+            stats(value, j - 2 * q, s3.at[q], MID)
+
+        exchanged.append(share(6 + q, s3.at[q]))
+
     pltpu.make_async_copy(raw, raw, load_sem.at[4]).wait()
 
-    @pl.loop(0, WIDE // CH)
-    def _(j):
-        at = lanes_at(j)
-        cen, amp, shi, inv = get(CEN, 3, j), get(AMP, 3, j), get(SHI, 3, j), get(INV, 3, j)
-
-        def add(r, acc):
-            band = band_at(r)
-            centred = pre3[band, at] - cen
-            summed = centred * amp + shi + x[band, at].astype(F32)
-            sigma = sigmoid(summed)
-            value = summed * sigma
-            upstream = raw_rows(r, at) * (sigma + value * (1.0 - sigma))
-            g3[band, at] = value.astype(BF16)
-            up[band, at] = upstream
-            pre3[band, at] = centred
-            return (acc[0] + fold_rows(upstream), acc[1] + fold_rows(upstream * centred))
-
-        zero = jnp.zeros((8, CH), F32)
-        shift_sum, gain_sum = lax.fori_loop(0, SIDE, add, (zero, zero))
-        s4[b, :, at] = total(shift_sum)
-        s4[b, :, pl.ds(pl.multiple_of(WIDE + j * CH, CH), CH)] = total(gain_sum) * inv
+    written, sums = [], []
+    for q in range(QUARTERS):
+        exchanged[q].wait()
+        group_stats(s3.at[q], 3, q * MID)
+
+        @pl.loop(2 * q, 2 * q + 2)
+        def _(j, q=q):
+            at = lanes_at(j)
+            cen, amp, shi, inv = get(CEN, 3, j), get(AMP, 3, j), get(SHI, 3, j), get(INV, 3, j)
+
+            def add(r, acc):
+                band = band_at(r)
+                centred = pre3[band, at] - cen
+                summed = centred * amp + shi + x[band, at].astype(F32)
+                sigma = sigmoid(summed)
+                value = summed * sigma
+                upstream = raw_rows(r, at) * (sigma + value * (1.0 - sigma))
+                g3[band, at] = value.astype(BF16)
+                up[band, at] = upstream
+                pre3[band, at] = centred
+                return (acc[0] + fold_rows(upstream), acc[1] + fold_rows(upstream * centred))
+
+            zero = jnp.zeros((8, CH), F32)
+            shift_sum, gain_sum = lax.fori_loop(0, SIDE, add, (zero, zero))
+            s4[q, b, :, lanes_at(j - 2 * q)] = total(shift_sum)
+            s4[q, b, :, pl.ds(pl.multiple_of(MID + (j - 2 * q) * CH, CH), CH)] = total(gain_sum) * inv
+
+        sums.append(share(6 + QUARTERS + q, s4.at[q]))
+        at = pl.ds(q * MID, MID)
+        copy = pltpu.make_async_copy(g3.at[:, at], out_hbm.at[:, at], out_sem.at[q])
+        copy.start()
+        written.append(copy)
 
     def turn(value):
         halves = value.T.reshape(16, 2, 16, ROWS)
@@ -484,24 +498,24 @@
     def sum_of(slots):
         return slots[0] + slots[1] + slots[2] + slots[3]
 
-    sums = share(3, s4)
-    write_out = pltpu.make_async_copy(g3, out_hbm, out_sem.at[0])
-    write_out.start()
-    turn(h2[...])
-    sums.wait()
-    group_sums(s4, 3)
-    write_out.wait()
-
-    @pl.loop(0, WIDE // CH)
-    def _(j):
-        at = lanes_at(j)
-        amp, ss, gs = get(AMP, 3, j), get(SS, 3, j), get(GS, 3, j)
-
-        @pl.loop(0, SIDE)
-        def _(r):
-            band = band_at(r)
-            grad = amp * (up[band, at] - ss - pre3[band, at] * gs)
-            g3[band, at] = real_rows(grad).astype(BF16)
+    def grad_three(q):
+        sums[q].wait()
+        group_sums(s4.at[q], 3, q * MID)
+        written[q].wait()
+
+        @pl.loop(2 * q, 2 * q + 2)
+        def _(j):
+            at = lanes_at(j)
+            amp, ss, gs = get(AMP, 3, j), get(SS, 3, j), get(GS, 3, j)
+
+            @pl.loop(0, SIDE)
+            def _(r):
+                band = band_at(r)
+                grad = amp * (up[band, at] - ss - pre3[band, at] * gs)
+                g3[band, at] = real_rows(grad).astype(BF16)
+
+    def tell_partner():
+        pl.semaphore_signal(ready, inc=1, device_id=partner, device_id_type=MESH)
 
     def slope_sums(pre, which, j, slots):
         at = lanes_at(j)
@@ -526,6 +540,15 @@
         cen, amp, ss, gs = get(CEN, which, j), get(AMP, which, j), get(SS, which, j), get(GS, which, j)
         return real_rows(amp * (back[band, at] - ss - (pre[band, at] - cen) * gs))
 
+    turn(h2[...])
+    grad_three(0)
+    grad_three(1)
+    tell_partner()
+    pl.semaphore_wait(ready, 1)
+    weigh("expand", lambda i, half: g3[:, pl.ds(pl.multiple_of(i * MID + half * CH, CH), CH)])
+    grad_three(2)
+    grad_three(3)
+    tell_partner()
     @pl.loop(0, MID // CH)
     def _(j):
         back[:, lanes_at(j)] = dot(g3[...], wa[:, lanes_at(j)])
@@ -534,9 +557,7 @@
     load_wr = load(5, wr_hbm, wa)
 
     sums = share(4, s5)
-    pl.semaphore_signal(ready, inc=1, device_id=partner, device_id_type=MESH)
     pl.semaphore_wait(ready, 1)
-    weigh("expand", lambda i, half: g3[:, pl.ds(pl.multiple_of(i * MID + half * CH, CH), CH)])
     weigh("extra", lambda i, half: g3[:, pl.ds(pl.multiple_of(1024 + i * MID + half * CH, CH), CH)])
     step("expand", 0)
     sums.wait()
@@ -668,7 +689,7 @@
     third_step("first", 4)
     to_owners(range(1))
     input_gradient(3)
-    write_in = pltpu.make_async_copy(g3, ing_hbm, out_sem.at[1])
+    write_in = pltpu.make_async_copy(g3, ing_hbm, out_sem.at[QUARTERS])
     write_in.start()
     last[b] = own[xx, yy, :, owned(b)]
 
@@ -722,8 +743,8 @@
             v((6, 1, 3072), F32),
             v((GROUP, 1, 2 * MID), F32),
             v((GROUP, 1, 2 * MID), F32),
-            v((GROUP, 1, 2 * WIDE), F32),
-            v((GROUP, 1, 2 * WIDE), F32),
+            v((QUARTERS, GROUP, 1, 2 * MID), F32),
+            v((QUARTERS, GROUP, 1, 2 * MID), F32),
             v((GROUP, 1, 2 * MID), F32),
             v((GROUP, 1, 2 * MID), F32),
             v((2, 3072), F32),
@@ -742,9 +763,9 @@
             v((4, 2, 3072), F32),
             v((4, 2, 3072), F32),
             dma((6 + SIDE,)),
-            dma((6,)),
-            dma((6,)),
-            dma((2,)),
+            dma((6 + 2 * QUARTERS,)),
+            dma((6 + 2 * QUARTERS,)),
+            dma((QUARTERS + 1,)),
             dma((SLOTS,)),
             dma((pieces,)),
             dma((pieces,)),

time: 103 us -> 98.7 us (0.958)
  Pallas kernels: 96.4 us -> 92 us
    pallas_call x1, Pallas kernels: 96.4 us -> 92 us  [run_block(): pl.pallas_call(block, out_shape=(jax.ShapeDtypeStruct((ROWS, WIDE), BF16)...]
where the time goes in v6:
time: 98.7 us; the launch traced here: 98.5 us
  Pallas kernels  92 us (93%)
  local copies, waits for them, and re-layouts  5.89 us (6%)
    pallas_call x1, Pallas kernels, run_block(): pl.pallas_call(block, out_shape=(jax.ShapeDtypeStruct((ROWS, WIDE), BF16)...  92 us
    transpose x1, local copies, waits for them, and re-layouts, from_rows(): rows.reshape(SIDE, IMGS, COLS, WIDE)[:, :, :SIDE].transpose(1, 0, 2, 3)  4.61 us

profile of v6, /device:TPU:0, one launch (start us, length us, event | category | flops | bytes accessed | tf_op | source)
XLA Modules:
  0.0 98.5 jit_solution(4593262109454306062)
XLA Ops:
  0.6 92.0 %block.1 = (bf16[672,2048]{1,0:T(8,128)(2,1)}, bf16[672,2048]{1,0:T(8,128)(2,1)}, f32[32,1088]{1,0:T(8,128)}, f32[2,3072]{1,0:T(2,128)}) custom-call(bf16[12,7,7,2048]{3,2,1,0:T(8,128)(2,1)} %x_hbm.1, bf16[12,7,7,2048]{3,2,1,0:T(8,128)(2,1)} %cot_hbm.1, bf16[2048,512]{1,0:T(8,128)(2,1)} %wr_hbm.1, bf16[4608,512]{1,0:T(8,128)(2,1)} %ws_hbm.1, ...), custom_call_target="tpu_custom_call" | custom-call | flops 17999998976 | bytes 40000000 | tf_op jit(solution)/shard_map/block/pallas_call | solution.py:717
  92.6 0.0 copy-start
  92.6 0.0 copy-start.1
  92.6 4.6 %copy_bitcast_fusion = (bf16[12,7,7,2048]{3,2,1,0:T(8,128)(2,1)}, bf16[12,7,7,2048]{3,2,1,0:T(8,128)(2,1)}) fusion(bf16[7,12,8,2048]{3,2,1,0:T(8,128)(2,1)} %bitcast.9, bf16[7,12,8,2048]{3,2,1,0:T(8,128)(2,1)} %bitcast.10), kind=kLoop, calls=%fused_computation | loop fusion | bytes 10321920 | tf_op jit(solution)/shard_map/transpose | solution.py:790
  97.2 0.0 copy-done
  97.2 0.7 copy.19
  97.9 0.0 copy-done.1
  97.9 0.6 copy.20
Async XLA Ops:
  92.6 4.6 %copy-start = (f32[32,1088]{1,0:T(8,128)S(1)}, f32[32,1088]{1,0:T(8,128)}, u32[]{:S(2)}) copy-start(f32[32,1088]{1,0:T(8,128)} %get-tuple-element.10) | copy-start | bytes 417796
  92.6 5.3 %copy-start.1 = (f32[2,3072]{1,0:T(2,128)S(1)}, f32[2,3072]{1,0:T(2,128)}, u32[]{:S(2)}) copy-start(f32[2,3072]{1,0:T(2,128)} %get-tuple-element.21) | copy-start | bytes 73732

commit v7 on v6

--- a/solution.py
+++ b/solution.py
@@ -560,6 +560,8 @@
     pl.semaphore_wait(ready, 1)
     weigh("extra", lambda i, half: g3[:, pl.ds(pl.multiple_of(1024 + i * MID + half * CH, CH), CH)])
     step("expand", 0)
+    third_step("expand", 0)
+    step("extra", 0)
     sums.wait()
     group_sums(s5, 2)
     @pl.loop(0, MID // CH)
@@ -596,28 +598,29 @@
 
     turn(g2[BAND : ROWS + BAND, MID : 2 * MID])
     weigh("low", tap_row(0))
-    step("extra", 0)
+    step("expand", 1)
     weigh("mid", tap_row(1))
-    step("expand", 1)
     step("low", 0)
-    third_step("expand", 0)
     third_step("low", 0)
+    step("extra", 1)
     weigh("high", tap_row(2))
+    third_step("expand", 1)
     step("mid", 0)
-    third_step("mid", 0)
-    step("extra", 1)
+    step("expand", 2)
     back_one(0)
     step("low", 1)
+    third_step("mid", 0)
     third_step("low", 1)
     step("high", 0)
     back_one(1)
+    step("expand", 3)
     sums = share(5, s6)
+    third_step("expand", 2)
+    third_step("high", 0)
+    step("mid", 1)
+    third_step("mid", 1)
+    step("high", 1)
     step("extra", 2)
-    step("mid", 1)
-    step("expand", 2)
-    third_step("mid", 1)
-    third_step("high", 0)
-    third_step("expand", 1)
     step("low", 2)
     sums.wait()
     group_sums(s6, 1)
@@ -630,57 +633,54 @@
         def _(r):
             h2[band_at(r), lanes_at(j)] = norm_back(pre1, 1, j, r).astype(BF16)
 
-    step("extra", 3)
-    step("high", 1)
-    third_step("low", 2)
+    third_step("high", 1)
     turn(h2[...])
     weigh("upper", lambda i, half: x[:, pl.ds(pl.multiple_of(1024 + i * MID + half * CH, CH), CH)])
+    third_step("expand", 3)
+    weigh("first", lambda i, half: x[:, pl.ds(pl.multiple_of(i * MID + half * CH, CH), CH)])
+    third_step("low", 2)
     third_step("mid", 2)
-    weigh("first", lambda i, half: x[:, pl.ds(pl.multiple_of(i * MID + half * CH, CH), CH)])
     step("upper", 0)
     third_step("upper", 0)
-    load_wr.wait()
-    input_gradient(0)
-    third_step("high", 1)
-    step("expand", 3)
-    step("mid", 2)
     step("first", 0)
-    step("high", 2)
-    third_step("first", 0)
-    third_step("upper", 1)
-    step("low", 3)
-    third_step("expand", 2)
-    third_step("mid", 3)
-    input_gradient(1)
-    step("mid", 3)
-    third_step("low", 3)
-    third_step("high", 2)
-    input_gradient(2)
-    step("expand", 4)
-    step("first", 1)
-    step("low", 4)
-    step("extra", 4)
     norm_copies.wait()
     nx[xx] = sum_of(ny)
     norm_copies = gather(1, "x", nx, xx)
+    step("mid", 2)
+    third_step("first", 0)
+    step("extra", 3)
+    step("low", 3)
+    third_step("expand", 4)
+    step("high", 2)
+    third_step("upper", 1)
+    step("expand", 4)
+    third_step("low", 3)
+    third_step("high", 2)
+    third_step("mid", 3)
+    third_step("first", 1)
     step("upper", 1)
-    third_step("first", 1)
+    step("mid", 3)
+    load_wr.wait()
+    input_gradient(0)
+    step("first", 1)
+    third_step("upper", 2)
     step("high", 3)
-    third_step("upper", 2)
+    input_gradient(1)
+    step("low", 4)
+    third_step("high", 3)
+    third_step("first", 2)
     third_step("mid", 4)
     step("mid", 4)
-    third_step("high", 3)
     third_step("low", 4)
     to_owners(range(2, 4))
-    third_step("expand", 3)
-    third_step("first", 2)
+    input_gradient(2)
     step("upper", 2)
+    step("extra", 4)
+    third_step("upper", 3)
+    step("high", 4)
     third_step("high", 4)
-    third_step("expand", 4)
-    step("high", 4)
+    step("first", 2)
     to_owners(range(4, GROUP))
-    third_step("upper", 3)
-    step("first", 2)
     third_step("first", 3)
     step("upper", 3)
     third_step("upper", 4)

time: 98.7 us -> 97.9 us (level)
  no operation moved by 1% of the time
where the time goes in v7:
time: 97.9 us; the launch traced here: 97.7 us
  Pallas kernels  91.1 us (93%)
  local copies, waits for them, and re-layouts  5.89 us (6%)
    pallas_call x1, Pallas kernels, run_block(): pl.pallas_call(block, out_shape=(jax.ShapeDtypeStruct((ROWS, WIDE), BF16)...  91.1 us
    transpose x1, local copies, waits for them, and re-layouts, from_rows(): rows.reshape(SIDE, IMGS, COLS, WIDE)[:, :, :SIDE].transpose(1, 0, 2, 3)  4.61 us

profile of v7, /device:TPU:0, one launch (start us, length us, event | category | flops | bytes accessed | tf_op | source)
XLA Modules:
  0.0 97.7 jit_solution(2491211965682256069)
XLA Ops:
  0.6 91.1 %block.1 = (bf16[672,2048]{1,0:T(8,128)(2,1)}, bf16[672,2048]{1,0:T(8,128)(2,1)}, f32[32,1088]{1,0:T(8,128)}, f32[2,3072]{1,0:T(2,128)}) custom-call(bf16[12,7,7,2048]{3,2,1,0:T(8,128)(2,1)} %x_hbm.1, bf16[12,7,7,2048]{3,2,1,0:T(8,128)(2,1)} %cot_hbm.1, bf16[2048,512]{1,0:T(8,128)(2,1)} %wr_hbm.1, bf16[4608,512]{1,0:T(8,128)(2,1)} %ws_hbm.1, ...), custom_call_target="tpu_custom_call" | custom-call | flops 17999998976 | bytes 40000000 | tf_op jit(solution)/shard_map/block/pallas_call | solution.py:717
  91.8 0.0 copy-start
  91.8 0.0 copy-start.1
  91.8 4.6 %copy_bitcast_fusion = (bf16[12,7,7,2048]{3,2,1,0:T(8,128)(2,1)}, bf16[12,7,7,2048]{3,2,1,0:T(8,128)(2,1)}) fusion(bf16[7,12,8,2048]{3,2,1,0:T(8,128)(2,1)} %bitcast.9, bf16[7,12,8,2048]{3,2,1,0:T(8,128)(2,1)} %bitcast.10), kind=kLoop, calls=%fused_computation | loop fusion | bytes 10321920 | tf_op jit(solution)/shard_map/transpose | solution.py:790
  96.4 0.0 copy-done
  96.4 0.7 copy.19
  97.1 0.0 copy-done.1
  97.1 0.6 copy.20
Async XLA Ops:
  91.8 4.6 %copy-start = (f32[32,1088]{1,0:T(8,128)S(1)}, f32[32,1088]{1,0:T(8,128)}, u32[]{:S(2)}) copy-start(f32[32,1088]{1,0:T(8,128)} %get-tuple-element.10) | copy-start | bytes 417796
  91.8 5.3 %copy-start.1 = (f32[2,3072]{1,0:T(2,128)S(1)}, f32[2,3072]{1,0:T(2,128)}, u32[]{:S(2)}) copy-start(f32[2,3072]{1,0:T(2,128)} %get-tuple-element.21) | copy-start | bytes 73732
